TPU v7x, 256 devices: a whole 4x4x8 slice. The times are simulated.
256 devices in a mesh: rep: 2 (over core), dp: 128 (over x, y, z).
Axes of the slice: x: 4, y: 4, z: 8, core: 2. Of those that a mesh axis runs over, the one named last changes fastest.
Arguments:
- x: bfloat16 [256, 2048, 640], P(('rep', 'dp')), parts along dimension 0
- dy: bfloat16 [256, 2048, 640], P(('rep', 'dp')), parts along dimension 0
- w_gate: bfloat16 [2, 640, 3200], P(None, 'dp')
- w_up: bfloat16 [2, 640, 3200], P(None, 'dp')
- w_down: bfloat16 [2, 3200, 640], P(None, 'dp')
Outputs:
- output 1: bfloat16 [256, 2048, 640], P(('rep', 'dp')), parts along dimension 0
- output 2: bfloat16 [4, 640, 3200], P('rep', 'dp'), parts along dimension 0
- output 3: bfloat16 [4, 640, 3200], P('rep', 'dp'), parts along dimension 0
- output 4: bfloat16 [4, 3200, 640], P('rep', 'dp'), parts along dimension 0
There are 2 independent parts. A program takes and returns all parts, laid end to end along the dimension named above; an argument that names none is the same for every part.
All inputs are finite; a program needn't handle non-finite values.
Results may differ from a plain program's by a relative error of at most 0.018.
Values are sent between devices in bfloat16 or wider.
A program may use at most 768 MiB of HBM per device.

v0:
```python
import jax
import jax.numpy as jnp
from jax import lax

NAMES = ("w_gate", "w_up", "w_down")


def matmul(a, w):
    return jnp.dot(a, w, preferred_element_type=jnp.float32).astype(jnp.bfloat16)


def normed(h):
    wide = h.astype(jnp.float32)
    scale = lax.rsqrt(jnp.mean(wide**2, -1, keepdims=True) + 1e-6)
    return (wide * scale).astype(jnp.bfloat16)


def layer(h, w):
    a = normed(h)
    gate = jnp.dot(a, w["w_gate"], preferred_element_type=jnp.float32)
    up = jnp.dot(a, w["w_up"], preferred_element_type=jnp.float32)
    return h + matmul((jax.nn.silu(gate) * up).astype(jnp.bfloat16), w["w_down"])


def stack(weights, h):
    for number in range(weights["w_gate"].shape[0]):
        h = layer(h, {name: w[number] for name, w in weights.items()})
    return h


def solution(mesh):
    groups = mesh.shape["rep"]

    def step(x, dy, *weights):
        shape = x.shape
        x, dy = (t.reshape(groups, -1, *t.shape[1:]) for t in (x, dy))

        def of_a_group(x, dy):
            _, back = jax.vjp(stack, dict(zip(NAMES, weights, strict=True)), x)
            by_weights, by_x = back(dy)
            return (by_x, *(by_weights[name] for name in NAMES))

        by_x, *by_weights = jax.vmap(of_a_group)(x, dy)
        return (by_x.reshape(shape), *(t.reshape(-1, *t.shape[2:]) for t in by_weights))

    return step
```

profile of v0, /device:TPU:32, one launch (start us, length us, event | category | flops | bytes accessed | tf_op | source)
XLA Modules:
  0.0 2513.8 jit_solution(8013139716297662305)
XLA Ops:
  26.8 111.0 %all-gather.29.cloned.1.call-done = bf16[1,640,3200]{2,0,1:T(2,128)(2,1)} async-done(((bf16[1,5,3200]{2,0,1:T(2,128)(2,1)}), bf16[1,640,3200]{2,0,1:T(2,128)(2,1)}) %all-gather.29.cloned.1.call-update) | async-done | bytes 4096016 | tf_op jit(solution)/vmap(jvp())/squeeze | solution.py:27
  137.8 19.5 fusion.71
  157.4 105.3 %all-gather.31.cloned.1.call-done = bf16[1,640,3200]{2,0,1:T(2,128)(2,1)} async-done(((bf16[1,5,3200]{2,0,1:T(2,128)(2,1)}), bf16[1,640,3200]{2,0,1:T(2,128)(2,1)}) %all-gather.31.cloned.1.call-update) | async-done | bytes 4096016 | tf_op jit(solution)/vmap(jvp())/squeeze | solution.py:27
  262.7 19.5 fusion.67
  282.1 22.9 fusion.26
  305.0 81.9 %all-gather.33.cloned.1.call-done = bf16[1,3200,640]{2,0,1:T(2,128)(2,1)} async-done(((bf16[1,25,640]{2,0,1:T(2,128)(2,1)}), bf16[1,3200,640]{2,0,1:T(2,128)(2,1)}) %all-gather.33.cloned.1.call-update) | async-done | bytes 4096016 | tf_op jit(solution)/vmap(jvp())/squeeze | solution.py:27
  386.9 16.0 fusion.51
  403.6 108.0 %all-gather.35.cloned.1.call-done = bf16[1,640,3200]{2,0,1:T(2,128)(2,1)} async-done(((bf16[1,5,3200]{2,0,1:T(2,128)(2,1)}), bf16[1,640,3200]{2,0,1:T(2,128)(2,1)}) %all-gather.35.cloned.1.call-update) | async-done | bytes 4096016 | tf_op jit(solution)/vmap(jvp())/squeeze | solution.py:27
  511.6 19.5 fusion.61
  531.1 105.2 %all-gather.39.cloned.1.call-done = bf16[1,640,3200]{2,0,1:T(2,128)(2,1)} async-done(((bf16[1,5,3200]{2,0,1:T(2,128)(2,1)}), bf16[1,640,3200]{2,0,1:T(2,128)(2,1)}) %all-gather.39.cloned.1.call-update) | async-done | bytes 4096016 | tf_op jit(solution)/vmap(jvp())/squeeze | solution.py:27
  636.3 17.9 fusion.54
  654.1 23.8 fusion.40
  677.9 82.5 %all-gather.37.cloned.1.call-done = bf16[1,3200,640]{2,0,1:T(2,128)(2,1)} async-done(((bf16[1,25,640]{2,0,1:T(2,128)(2,1)}), bf16[1,3200,640]{2,0,1:T(2,128)(2,1)}) %all-gather.37.cloned.1.call-update) | async-done | bytes 4096016 | tf_op jit(solution)/vmap(jvp())/squeeze | solution.py:27
  760.4 17.4 convolution_convert_fusion.1
  777.8 27.0 %fusion.6 = bf16[2048,3200]{1,0:T(8,128)(2,1)} fusion(f32[2048,3200]{1,0:T(8,128)} %fusion.61, f32[2048,3200]{1,0:T(8,128)} %fusion.54, bf16[2048,3200]{1,0:T(8,128)(2,1)} %convolution_convert_fusion.1), kind=kLoop, calls=%fused_computation.10 | loop fusion | flops 78643200 | bytes 78643200
  804.8 15.5 fusion.79
  820.3 20.7 fusion.53
  842.9 16.8 convolution_bitcast_fusion
  859.8 409.4 %fusion.158 = (f32[32,640]{1,0:T(8,128)}, f32[32,640]{1,0:T(8,128)S(1)}) fusion(f32[1,3200,640]{2,1,0:T(8,128)} %convolution_bitcast_fusion, f32[1,3200,640]{2,1,0:T(8,128)} %fusion.40), kind=kCustom, calls=%all-reduce-scatter.2 | all-reduce-scatter fusion | flops 5242881 | bytes 16548864
  1277.5 20.5 fusion.34
  1299.3 16.9 convolution_convert_fusion
  1316.1 26.9 %fusion.9 = bf16[2048,3200]{1,0:T(8,128)(2,1)} fusion(f32[2048,3200]{1,0:T(8,128)} %fusion.71, f32[2048,3200]{1,0:T(8,128)} %fusion.67, bf16[2048,3200]{1,0:T(8,128)(2,1)} %convolution_convert_fusion), kind=kLoop, calls=%fused_computation.13 | loop fusion | flops 78643200 | bytes 78643200
  1343.1 14.6 fusion.73
  1357.7 19.6 fusion.49
  1381.6 16.2 collective-permute-start.13
  1420.4 19.8 fusion.37
  1460.4 14.7 convolution_bitcast_fusion.1
  1483.5 14.9 convolution_bitcast_fusion.2
  1514.2 855.3 %all-reduce.17 = (bf16[1,640,3200]{2,1,0:T(8,128)(2,1)}, bf16[1,640,3200]{2,1,0:T(8,128)(2,1)}, bf16[1,640,3200]{2,1,0:T(8,128)(2,1)}, bf16[1,640,3200]{2,1,0:T(8,128)(2,1)}) all-reduce(f32[1,640,3200]{2,1,0:T(8,128)} %convolution_bitcast_fusion.1, f32[1,640,3200]{2,1,0:T(8,128)} %convolution_bitcast_fusion.2, ...), channel_id=25, replica_groups=[2,128]<=[256], use_global_device_ids=true, to_apply=%add.1.clone.clone | all-reduce | flops 8192000 | bytes 49152000
  2400.3 26.8 %collective-permute-start.40 = (bf16[32,640]{1,0:T(8,128)(2,1)S(1)}, bf16[32,640]{1,0:T(8,128)(2,1)S(1)}, u32[]{:S(2)}, u32[]{:S(2)}) collective-permute-start(bf16[32,640]{1,0:T(8,128)(2,1)S(1)} %convert.174), channel_id=1, source_target_pairs={{0,13},{1,14},{2,15},{3,16},{4,17},{5,18},{6,19},{7,20},{8,21},{9,... | collective-permute-start | bytes 122888
  2427.1 22.5 collective-permute-start.41
  2473.9 13.7 concatenate
  (201 shorter events, 174.9 us)
Async XLA Ops:
  7.2 130.7 %all-gather.29.cloned.1.call-start = ((), (), s32[]{:S(2)}) async-start(), calls=%async_computation | async-start | bytes 8256000 | tf_op jit(solution)/vmap(jvp())/squeeze | solution.py:27
  8.9 253.7 %all-gather.31.cloned.1.call-start = ((), (), s32[]{:S(2)}) async-start(), calls=%async_computation.1 | async-start | bytes 8256000 | tf_op jit(solution)/vmap(jvp())/squeeze | solution.py:27
  10.7 376.2 %all-gather.33.cloned.1.call-start = ((), (), s32[]{:S(2)}) async-start(), calls=%async_computation.2 | async-start | bytes 8256000 | tf_op jit(solution)/vmap(jvp())/squeeze | solution.py:27
  12.4 499.1 %all-gather.35.cloned.1.call-start = ((), (), s32[]{:S(2)}) async-start(), calls=%async_computation.3 | async-start | bytes 8256000 | tf_op jit(solution)/vmap(jvp())/squeeze | solution.py:27
  13.0 623.2 %all-gather.39.cloned.1.call-start = ((), (), s32[]{:S(2)}) async-start(), calls=%async_computation.5 | async-start | bytes 8256000 | tf_op jit(solution)/vmap(jvp())/squeeze | solution.py:27
  13.6 746.8 %all-gather.37.cloned.1.call-start = ((), (), s32[]{:S(2)}) async-start(), calls=%async_computation.4 | async-start | bytes 8256000 | tf_op jit(solution)/vmap(jvp())/squeeze | solution.py:27
  1269.8 111.7 %collective-permute-start = (bf16[32,640]{1,0:T(8,128)(2,1)}, bf16[32,640]{1,0:T(8,128)(2,1)}, u32[]{:S(2)}, u32[]{:S(2)}) collective-permute-start(bf16[32,640]{1,0:T(8,128)(2,1)} %convert.173), channel_id=1, source_target_pairs={{0,1},{1,2},{2,3},{3,4},{4,5},{5,6},{6,7},{7,8},{8,9},{9,10},{10,1... | collective-permute-start | bytes 122888
  1271.8 126.0 %collective-permute-start.1 = (bf16[32,640]{1,0:T(8,128)(2,1)}, bf16[32,640]{1,0:T(8,128)(2,1)}, u32[]{:S(2)}, u32[]{:S(2)}) collective-permute-start(bf16[32,640]{1,0:T(8,128)(2,1)} %convert.173), channel_id=1, source_target_pairs={{0,2},{1,3},{2,4},{3,5},{4,6},{5,7},{6,8},{7,9},{8,10},{9,11},{10,... | collective-permute-start | bytes 122888
  1273.7 134.9 %collective-permute-start.10 = (bf16[32,640]{1,0:T(8,128)(2,1)}, bf16[32,640]{1,0:T(8,128)(2,1)}, u32[]{:S(2)}, u32[]{:S(2)}) collective-permute-start(bf16[32,640]{1,0:T(8,128)(2,1)} %convert.173), channel_id=1, source_target_pairs={{0,11},{1,12},{2,13},{3,14},{4,15},{5,16},{6,17},{7,18},{8,19},{9,... | collective-permute-start | bytes 122888
  1275.6 138.3 %collective-permute-start.11 = (bf16[32,640]{1,0:T(8,128)(2,1)}, bf16[32,640]{1,0:T(8,128)(2,1)}, u32[]{:S(2)}, u32[]{:S(2)}) collective-permute-start(bf16[32,640]{1,0:T(8,128)(2,1)} %convert.173), channel_id=1, source_target_pairs={{0,12},{1,13},{2,14},{3,15},{4,16},{5,17},{6,18},{7,19},{8,20},{9,... | collective-permute-start | bytes 122888
  1298.0 79.3 %collective-permute-start.27 = (bf16[25,640]{1,0:T(8,128)(2,1)S(1)}, bf16[25,640]{1,0:T(8,128)(2,1)S(1)}, u32[]{:S(2)}, u32[]{:S(2)}) collective-permute-start(bf16[25,640]{1,0:T(8,128)(2,1)S(1)} %slice.24), channel_id=1, source_target_pairs={{0,28},{1,29},{2,30},{3,31},{4,32},{5,33},{6,34},{7,35},{8,36},{9,... | collective-permute-start | bytes 96008
  1380.3 60.0 %collective-permute-start.12 = (bf16[32,640]{1,0:T(8,128)(2,1)}, bf16[32,640]{1,0:T(8,128)(2,1)S(1)}, u32[]{:S(2)}, u32[]{:S(2)}) collective-permute-start(bf16[32,640]{1,0:T(8,128)(2,1)} %convert.173), channel_id=1, source_target_pairs={{0,13},{1,14},{2,15},{3,16},{4,17},{5,18},{6,19},{7,20},{8,21},{9,... | collective-permute-start | bytes 122888
  1381.6 60.2 %collective-permute-start.13 = (bf16[32,640]{1,0:T(8,128)(2,1)}, bf16[32,640]{1,0:T(8,128)(2,1)S(1)}, u32[]{:S(2)}, u32[]{:S(2)}) collective-permute-start(bf16[32,640]{1,0:T(8,128)(2,1)} %convert.173), channel_id=1, source_target_pairs={{0,14},{1,15},{2,16},{3,17},{4,18},{5,19},{6,20},{7,21},{8,22},{9,... | collective-permute-start | bytes 122888
  1397.8 51.3 %collective-permute-start.14 = (bf16[32,640]{1,0:T(8,128)(2,1)}, bf16[32,640]{1,0:T(8,128)(2,1)S(1)}, u32[]{:S(2)}, u32[]{:S(2)}) collective-permute-start(bf16[32,640]{1,0:T(8,128)(2,1)} %convert.173), channel_id=1, source_target_pairs={{0,15},{1,16},{2,17},{3,18},{4,19},{5,20},{6,21},{7,22},{8,23},{9,... | collective-permute-start | bytes 122888
  1408.6 45.5 %collective-permute-start.15 = (bf16[32,640]{1,0:T(8,128)(2,1)}, bf16[32,640]{1,0:T(8,128)(2,1)S(1)}, u32[]{:S(2)}, u32[]{:S(2)}) collective-permute-start(bf16[32,640]{1,0:T(8,128)(2,1)} %convert.173), channel_id=1, source_target_pairs={{0,16},{1,17},{2,18},{3,19},{4,20},{5,21},{6,22},{7,23},{8,24},{9,... | collective-permute-start | bytes 122888
  1413.8 44.6 %collective-permute-start.16 = (bf16[32,640]{1,0:T(8,128)(2,1)}, bf16[32,640]{1,0:T(8,128)(2,1)S(1)}, u32[]{:S(2)}, u32[]{:S(2)}) collective-permute-start(bf16[32,640]{1,0:T(8,128)(2,1)} %convert.173), channel_id=1, source_target_pairs={{0,17},{1,18},{2,19},{3,20},{4,21},{5,22},{6,23},{7,24},{8,25},{9,... | collective-permute-start | bytes 122888
  1440.2 34.9 %collective-permute-start.17 = (bf16[32,640]{1,0:T(8,128)(2,1)}, bf16[32,640]{1,0:T(8,128)(2,1)S(1)}, u32[]{:S(2)}, u32[]{:S(2)}) collective-permute-start(bf16[32,640]{1,0:T(8,128)(2,1)} %convert.173), channel_id=1, source_target_pairs={{0,18},{1,19},{2,20},{3,21},{4,22},{5,23},{6,24},{7,25},{8,26},{9,... | collective-permute-start | bytes 122888
  1441.8 34.8 %collective-permute-start.18 = (bf16[32,640]{1,0:T(8,128)(2,1)}, bf16[32,640]{1,0:T(8,128)(2,1)S(1)}, u32[]{:S(2)}, u32[]{:S(2)}) collective-permute-start(bf16[32,640]{1,0:T(8,128)(2,1)} %convert.173), channel_id=1, source_target_pairs={{0,19},{1,20},{2,21},{3,22},{4,23},{5,24},{6,25},{7,26},{8,27},{9,... | collective-permute-start | bytes 122888
  1480.2 29.4 %collective-permute-start.24 = (bf16[32,640]{1,0:T(8,128)(2,1)}, bf16[32,640]{1,0:T(8,128)(2,1)S(1)}, u32[]{:S(2)}, u32[]{:S(2)}) collective-permute-start(bf16[32,640]{1,0:T(8,128)(2,1)} %convert.173), channel_id=1, source_target_pairs={{0,25},{1,26},{2,27},{3,28},{4,29},{5,30},{6,31},{7,32},{8,33},{9,... | collective-permute-start | bytes 122888
  1482.2 29.4 %collective-permute-start.25 = (bf16[32,640]{1,0:T(8,128)(2,1)}, bf16[32,640]{1,0:T(8,128)(2,1)S(1)}, u32[]{:S(2)}, u32[]{:S(2)}) collective-permute-start(bf16[32,640]{1,0:T(8,128)(2,1)} %convert.173), channel_id=1, source_target_pairs={{0,26},{1,27},{2,28},{3,29},{4,30},{5,31},{6,32},{7,33},{8,34},{9,... | collective-permute-start | bytes 122888
  1498.4 871.1 %collective-permute-start.26 = (bf16[32,640]{1,0:T(8,128)(2,1)}, bf16[32,640]{1,0:T(8,128)(2,1)S(1)}, u32[]{:S(2)}, u32[]{:S(2)}) collective-permute-start(bf16[32,640]{1,0:T(8,128)(2,1)} %convert.173), channel_id=1, source_target_pairs={{0,27},{1,28},{2,29},{3,30},{4,31},{5,32},{6,33},{7,34},{8,35},{9,... | collective-permute-start | bytes 122888
  1500.6 870.2 %collective-permute-start.3 = (bf16[32,640]{1,0:T(8,128)(2,1)}, bf16[32,640]{1,0:T(8,128)(2,1)S(1)}, u32[]{:S(2)}, u32[]{:S(2)}) collective-permute-start(bf16[32,640]{1,0:T(8,128)(2,1)} %convert.173), channel_id=1, source_target_pairs={{0,4},{1,5},{2,6},{3,7},{4,8},{5,9},{6,10},{7,11},{8,12},{9,13},{1... | collective-permute-start | bytes 122888
  1504.9 867.3 %collective-permute-start.4 = (bf16[32,640]{1,0:T(8,128)(2,1)}, bf16[32,640]{1,0:T(8,128)(2,1)}, u32[]{:S(2)}, u32[]{:S(2)}) collective-permute-start(bf16[32,640]{1,0:T(8,128)(2,1)} %convert.173), channel_id=1, source_target_pairs={{0,5},{1,6},{2,7},{3,8},{4,9},{5,10},{6,11},{7,12},{8,13},{9,14},{... | collective-permute-start | bytes 122888
  1509.6 863.9 %collective-permute-start.5 = (bf16[32,640]{1,0:T(8,128)(2,1)}, bf16[32,640]{1,0:T(8,128)(2,1)}, u32[]{:S(2)}, u32[]{:S(2)}) collective-permute-start(bf16[32,640]{1,0:T(8,128)(2,1)} %convert.173), channel_id=1, source_target_pairs={{0,6},{1,7},{2,8},{3,9},{4,10},{5,11},{6,12},{7,13},{8,14},{9,15},... | collective-permute-start | bytes 122888
  1511.5 864.5 %collective-permute-start.6 = (bf16[32,640]{1,0:T(8,128)(2,1)}, bf16[32,640]{1,0:T(8,128)(2,1)}, u32[]{:S(2)}, u32[]{:S(2)}) collective-permute-start(bf16[32,640]{1,0:T(8,128)(2,1)} %convert.173), channel_id=1, source_target_pairs={{0,7},{1,8},{2,9},{3,10},{4,11},{5,12},{6,13},{7,14},{8,15},{9,16}... | collective-permute-start | bytes 122888
  2395.0 32.1 %collective-permute-start.36 = (bf16[32,640]{1,0:T(8,128)(2,1)S(1)}, bf16[32,640]{1,0:T(8,128)(2,1)S(1)}, u32[]{:S(2)}, u32[]{:S(2)}) collective-permute-start(bf16[32,640]{1,0:T(8,128)(2,1)S(1)} %convert.174), channel_id=1, source_target_pairs={{0,9},{1,10},{2,11},{3,12},{4,13},{5,14},{6,15},{7,16},{8,17},{9,1... | collective-permute-start | bytes 122888
  2396.3 53.3 %collective-permute-start.37 = (bf16[32,640]{1,0:T(8,128)(2,1)S(1)}, bf16[32,640]{1,0:T(8,128)(2,1)S(1)}, u32[]{:S(2)}, u32[]{:S(2)}) collective-permute-start(bf16[32,640]{1,0:T(8,128)(2,1)S(1)} %convert.174), channel_id=1, source_target_pairs={{0,10},{1,11},{2,12},{3,13},{4,14},{5,15},{6,16},{7,17},{8,18},{9,... | collective-permute-start | bytes 122888
  2397.6 55.2 %collective-permute-start.38 = (bf16[32,640]{1,0:T(8,128)(2,1)S(1)}, bf16[32,640]{1,0:T(8,128)(2,1)S(1)}, u32[]{:S(2)}, u32[]{:S(2)}) collective-permute-start(bf16[32,640]{1,0:T(8,128)(2,1)S(1)} %convert.174), channel_id=1, source_target_pairs={{0,11},{1,12},{2,13},{3,14},{4,15},{5,16},{6,17},{7,18},{8,19},{9,... | collective-permute-start | bytes 122888
  2398.9 55.8 %collective-permute-start.39 = (bf16[32,640]{1,0:T(8,128)(2,1)S(1)}, bf16[32,640]{1,0:T(8,128)(2,1)S(1)}, u32[]{:S(2)}, u32[]{:S(2)}) collective-permute-start(bf16[32,640]{1,0:T(8,128)(2,1)S(1)} %convert.174), channel_id=1, source_target_pairs={{0,12},{1,13},{2,14},{3,15},{4,16},{5,17},{6,18},{7,19},{8,20},{9,... | collective-permute-start | bytes 122888
  2400.3 56.8 %collective-permute-start.40 = (bf16[32,640]{1,0:T(8,128)(2,1)S(1)}, bf16[32,640]{1,0:T(8,128)(2,1)S(1)}, u32[]{:S(2)}, u32[]{:S(2)}) collective-permute-start(bf16[32,640]{1,0:T(8,128)(2,1)S(1)} %convert.174), channel_id=1, source_target_pairs={{0,13},{1,14},{2,15},{3,16},{4,17},{5,18},{6,19},{7,20},{8,21},{9,... | collective-permute-start | bytes 122888
  2427.1 32.5 %collective-permute-start.41 = (bf16[32,640]{1,0:T(8,128)(2,1)S(1)}, bf16[32,640]{1,0:T(8,128)(2,1)S(1)}, u32[]{:S(2)}, u32[]{:S(2)}) collective-permute-start(bf16[32,640]{1,0:T(8,128)(2,1)S(1)} %convert.174), channel_id=1, source_target_pairs={{0,14},{1,15},{2,16},{3,17},{4,18},{5,19},{6,20},{7,21},{8,22},{9,... | collective-permute-start | bytes 122888
  2457.1 30.5 %collective-permute-start.45 = (bf16[32,640]{1,0:T(8,128)(2,1)S(1)}, bf16[32,640]{1,0:T(8,128)(2,1)S(1)}, u32[]{:S(2)}, u32[]{:S(2)}) collective-permute-start(bf16[32,640]{1,0:T(8,128)(2,1)S(1)} %convert.174), channel_id=1, source_target_pairs={{0,18},{1,19},{2,20},{3,21},{4,22},{5,23},{6,24},{7,25},{8,26},{9,... | collective-permute-start | bytes 122888
  (55 other events, 3309.5 us)
Sparse Core Ops, SparseCore 0:
  12.2 125.6 all-gather.28
  142.0 120.5 all-gather.30
  266.3 120.5 all-gather.32
  390.9 120.5 all-gather.34
  515.6 120.5 all-gather.38
  639.7 120.5 all-gather.36
where the time goes:
time: 2530 us; the launch traced here: 2510 us
  blocking collectives  1260 us (50%)
  waiting for transfers between devices  600 us (24%)
  matrix products  308 us (12%)
  starting transfers between devices  193 us (8%)
  other arithmetic  88.3 us (3%)
  local copies, waits for them, and re-layouts  43.5 us (2%)
    unnamed x2, blocking collectives  1260 us
    squeeze x6, waiting for transfers between devices, stack(): h = layer(h, {name: w[number] for name, w in weights.items()})  594 us
    unnamed x56, starting transfers between devices  193 us
    dot_general x6, matrix products, layer(): up = jnp.dot(a, w['w_up'], preferred_element_type=jnp.float32)  118 us
    dot_general x6, matrix products, layer(): gate = jnp.dot(a, w['w_gate'], preferred_element_type=jnp.float32)  98.7 us
    dot_general x5, matrix products, matmul(): jnp.dot(a, w, preferred_element_type=jnp.float32).astype(jnp.bfloat16)  90.9 us
    unnamed x5, other arithmetic  77.5 us
  transfers between devices with their start and end apart: 62, of which 8 were waited for; matrix products, arithmetic and copies ran while one was open for 13% of the time, Pallas kernels for 0%

commit v1 on v0

v1 whole, which is shorter than its diff:
```python
import jax
import jax.numpy as jnp
from jax import lax
from jax.sharding import Mesh, PartitionSpec as P

F32, BF16 = jnp.float32, jnp.bfloat16


def dot(a, b, ca, cb):
    return lax.dot_general(a, b, (((ca,), (cb,)), ((), ())), preferred_element_type=F32)


def norm_parts(h):
    wide = h.astype(F32)
    scale = lax.rsqrt(jnp.mean(wide**2, -1, keepdims=True) + 1e-6)
    return wide, scale


def forward(h, wg, wu, wd, last):
    wide, scale = norm_parts(h)
    a = (wide * scale).astype(BF16)
    gate, up = dot(a, wg, 1, 0), dot(a, wu, 1, 0)
    p = (jax.nn.silu(gate) * up).astype(BF16)
    out = None if last else h + dot(p, wd, 1, 0).astype(BF16)
    return out, (wide, scale, a, gate, up, p)


def backward(d, saved, wg, wu, wd):
    wide, scale, a, gate, up, p = saved
    dp = dot(d, wd, 1, 1).astype(BF16).astype(F32)
    dwd = dot(p, d, 0, 0).astype(BF16)
    sig = jax.nn.sigmoid(gate)
    dg = (dp * up * (sig * (1 + gate * (1 - sig)))).astype(BF16)
    du = (dp * gate * sig).astype(BF16)
    dwg, dwu = dot(a, dg, 0, 0).astype(BF16), dot(a, du, 0, 0).astype(BF16)
    da = (dot(dg, wg, 1, 1).astype(BF16) + dot(du, wu, 1, 1).astype(BF16)).astype(F32)
    inner = jnp.sum(da * wide, -1, keepdims=True) / wide.shape[-1]
    dwide = da * scale - wide * (scale**3 * inner)
    return d + dwide.astype(BF16), dwg, dwu, dwd


def solution(mesh):
    groups, n = mesh.shape["rep"], mesh.shape["dp"]
    fine = Mesh(mesh.devices.reshape(groups, 4, 4, n // 16), ("rep", "x", "y", "z"))
    every = ("x", "y", "z")

    def step(x, dy, wg, wu, wd):
        d_model, ff = wg.shape[1] * n, wg.shape[2]
        wg0 = lax.all_gather(wg[0], every, axis=0, tiled=True)
        wu0 = lax.all_gather(wu[0].reshape(-1, 128), every, axis=0, tiled=True).reshape(d_model, ff)
        wd0 = wd[0]
        for axis in ("z", "y", "x"):
            wd0 = lax.all_gather(wd0, axis, axis=0, tiled=True)
        flat = jnp.concatenate([t[1].reshape(-1, 128) for t in (wg, wu, wd)])
        flat = lax.all_gather(flat, every, axis=0)
        cuts = (0, wg[1].size // 128, 2 * wg[1].size // 128, flat.shape[1])
        wg1, wu1, wd1 = (flat[:, lo:hi].reshape(s) for lo, hi, s in zip(cuts[:-1], cuts[1:], ((d_model, ff), (d_model, ff), (ff, d_model))))

        h0, dh = x[0], dy[0]
        h1, saved0 = forward(h0, wg0, wu0, wd0, False)
        _, saved1 = forward(h1, wg1, wu1, wd1, True)
        dh, g1, u1, d1 = backward(dh, saved1, wg1, wu1, wd1)
        flat = jnp.concatenate([t.reshape(n, -1, 128) for t in (g1, u1, d1)], 1)
        flat = flat.reshape(4, 4, -1, *flat.shape[1:])
        for axis in every:
            flat = lax.psum_scatter(flat, axis, scatter_dimension=0)
        g1, u1, d1 = (flat[lo:hi].reshape(s) for lo, hi, s in zip(cuts[:-1], cuts[1:], (wg.shape[1:], wu.shape[1:], wd.shape[1:])))
        dh, g0, u0, d0 = backward(dh, saved0, wg0, wu0, wd0)
        for axis in every:
            d0 = lax.psum_scatter(d0, axis, scatter_dimension=0, tiled=True)
        u0 = u0.reshape(16, -1, 128)
        u0 = lax.psum_scatter(u0, ("x", "y"), scatter_dimension=0)
        u0 = lax.psum_scatter(u0, "z", scatter_dimension=0, tiled=True).reshape(wu.shape[1:])
        for axis in ("x", "y", "z"):
            g0 = lax.psum_scatter(g0, axis, scatter_dimension=0, tiled=True)
        return dh[None], jnp.stack([g0, g1]), jnp.stack([u0, u1]), jnp.stack([d0, d1])

    data = P(("rep", *every), None, None)
    weight = P(None, every, None)
    grad = P("rep", every, None)
    return jax.shard_map(step, mesh=fine, in_specs=(data, data, weight, weight, weight), out_specs=(data, grad, grad, grad), check_vma=False)
```

time: 2530 us -> 1170 us (0.46)
  blocking collectives: 1260 us -> 65.6 us
  starting transfers between devices: 193 us -> 10.9 us
  other arithmetic: 88.3 us -> 22.9 us
  local copies, waits for them, and re-layouts: 43.5 us -> 93.9 us
  waiting for transfers between devices: 600 us -> 634 us
    unnamed x2 -> x1, blocking collectives: 1260 us -> 22.2 us
    squeeze x6 -> x0, waiting for transfers between devices: 594 us -> none  [stack(): h = layer(h, {name: w[number] for name, w in weights.items()})]
    all_gather x0 -> x4, waiting for transfers between devices: none -> 309 us  [the longest x1 123 us: step(): flat = lax.all_gather(flat, every, axis=0)]
    unnamed x56 -> x7, starting transfers between devices: 193 us -> 10.6 us
    unnamed x62 -> x19, waiting for transfers between devices: 5.94 us -> 175 us
    reduce_scatter x0 -> x4, waiting for transfers between devices: none -> 149 us  [the longest x2 140 us: step(): flat = lax.psum_scatter(flat, axis, scatter_dimension=0)]
    unnamed x5 -> x1, other arithmetic: 77.5 us -> 0.68 us
    all_gather x0 -> x2, blocking collectives: none -> 43.4 us  [step(): wd0 = lax.all_gather(wd0, axis, axis=0, tiled=True)]
  transfers between devices with their start and end apart: 62 -> 15, of which waited for: 8 -> 12; matrix products, arithmetic and copies ran while one was open for 13% -> 24% of each run, Pallas kernels for 0% -> 0%
where the time goes in v1:
time: 1170 us; the launch traced here: 1160 us
  waiting for transfers between devices  634 us (54%)
  matrix products  317 us (27%)
  local copies, waits for them, and re-layouts  93.9 us (8%)
  blocking collectives  65.6 us (6%)
  other arithmetic  22.9 us (2%)
  between operations  16.9 us (1%)
    dot_general x17, matrix products, dot(): lax.dot_general(a, b, (((ca,), (cb,)), ((), ())), preferred_element_type=...  317 us
    unnamed x19, waiting for transfers between devices  175 us
    reduce_scatter x2, waiting for transfers between devices, step(): flat = lax.psum_scatter(flat, axis, scatter_dimension=0)  140 us
    all_gather x1, waiting for transfers between devices, step(): flat = lax.all_gather(flat, every, axis=0)  123 us
    all_gather x1, waiting for transfers between devices, step(): wg0 = lax.all_gather(wg[0], every, axis=0, tiled=True)  117 us
    all_gather x1, waiting for transfers between devices, step(): lax.all_gather(wu[0].reshape(-1, 128), every, axis=0, tiled=True)  65.2 us
    all_gather x2, blocking collectives, step(): wd0 = lax.all_gather(wd0, axis, axis=0, tiled=True)  43.4 us
  transfers between devices with their start and end apart: 15, of which 12 were waited for; matrix products, arithmetic and copies ran while one was open for 24% of the time, Pallas kernels for 0%

profile of v1, /device:TPU:32, one launch (start us, length us, event | category | flops | bytes accessed | tf_op | source)
XLA Modules:
  0.0 1160.6 jit_solution(1235129923998135210)
XLA Ops:
  12.1 28.1 %all-gather.2 = bf16[1,200,640]{2,0,1:T(2,128)(2,1)S(1)} all-gather(bf16[1,25,640]{2,0,1:T(2,128)(2,1)S(1)} %get-tuple-element.37), channel_id=4, replica_groups=mesh['rep'=2,'x'=4,'y'=4,'z'=8] {'z'}, dimensions={1}, use_global_device_ids=true | all-gather | bytes 288000 | tf_op jit(solution)/shard_map/all_gather | solution.py:53
  40.2 15.2 %all-gather.3 = bf16[1,800,640]{2,1,0:T(8,128)(2,1)} all-gather(bf16[1,200,640]{2,1,0:T(8,128)(2,1)S(1)} %copy.53), channel_id=5, replica_groups=mesh['rep'=2,'x'=4,'y'=4,'z'=8] {'y'}, dimensions={1}, use_global_device_ids=true | all-gather | bytes 1280000 | tf_op jit(solution)/shard_map/all_gather | solution.py:53
  65.6 65.2 %all-gather.18.cloned.1.call-done = bf16[128,125,128]{2,1,0:T(8,128)(2,1)} async-done(((bf16[1,125,128]{2,1,0:T(8,128)(2,1)}), bf16[128,125,128]{2,1,0:T(8,128)(2,1)}) %all-gather.18.cloned.1.call-update) | async-done | bytes 4096016 | tf_op jit(solution)/shard_map/all_gather | solution.py:50
  138.4 117.5 %all-gather.12.cloned.1.call-done = bf16[1,640,3200]{2,0,1:T(2,128)(2,1)} async-done(((bf16[1,5,3200]{2,0,1:T(2,128)(2,1)}), bf16[1,640,3200]{2,0,1:T(2,128)(2,1)}) %all-gather.12.cloned.1.call-update) | async-done | bytes 4096016 | tf_op jit(solution)/shard_map/all_gather | solution.py:49
  255.9 17.3 %fusion.24 = f32[2048,3200]{0,1:T(8,128)} fusion(bf16[1,2048,640]{1,2,0:T(8,128)(2,1)S(1)} %copy.49, f32[2048]{0:T(1024)S(1)} %add_rsqrt_fusion.1, bf16[1,640,3200]{2,0,1:T(2,128)(2,1)} %all-gather.12.cloned.1.call-done), kind=kOutput, calls=%fused_computation.49 | convolution fusion | flops 8392540160 | bytes 32940032 | tf_op jit(solution)/shard_map/dot_general | solution.py:10
  273.2 28.1 %multiply_convert_fusion.1 = (bf16[2048,3200]{0,1:T(8,128)(2,1)}, f32[2048,3200]{0,1:T(8,128)}) fusion(f32[2048,3200]{0,1:T(8,128)} %fusion.24, bf16[640,3200]{1,0:T(8,128)(2,1)S(1)} %copy-done.3, bf16[1,2048,640]{2,1,0:T(8,128)(2,1)} %param.5, f32[2048]{0:T(1024)S(1)} %add_rsqrt_fusion.1), kind=kOutput, calls=%fused_computation.14 | convolution fusion | flops 8431861760 | bytes 72261632 | tf_op jit(solution)/shard_map/dot_general | solution.py:10
  305.1 14.8 %fusion.19 = (f32[2048]{0:T(1024)S(1)}, bf16[2048,640]{0,1:T(8,128)(2,1)}) fusion(bf16[2048,3200]{0,1:T(8,128)(2,1)} %get-tuple-element.40, bf16[1,3200,640]{2,1,0:T(8,128)(2,1)} %all-gather.14.cloned.1.call-done, bf16[1,2048,640]{1,2,0:T(8,128)(2,1)S(1)} %copy.49), kind=kOutput, calls=%fused_computation.43 | convolution fusion | flops 8395159552 | bytes 22454272 | tf_op jit(solution)/shard_map/dot_general | solution.py:10
  319.9 123.0 %all-gather.16.cloned.1.call-done = bf16[128,375,128]{2,1,0:T(8,128)(2,1)} async-done(((bf16[1,375,128]{2,1,0:T(8,128)(2,1)}), bf16[128,375,128]{2,1,0:T(8,128)(2,1)}) %all-gather.16.cloned.1.call-update) | async-done | bytes 12288016 | tf_op jit(solution)/shard_map/all_gather | solution.py:55
  442.9 9.2 fusion.64
  474.1 16.6 %convolution_convert_fusion.1 = bf16[3200,2048]{1,0:T(8,128)(2,1)} fusion(bf16[3200,640]{1,0:T(8,128)(2,1)} %reshape.87, bf16[1,2048,640]{2,1,0:T(8,128)(2,1)} %param.6), kind=kOutput, calls=%fused_computation.17 | convolution fusion | flops 8395161600 | bytes 19824640 | tf_op jit(solution)/shard_map/dot_general | solution.py:10
  490.8 13.9 %fusion.54 = f32[2048,3200]{0,1:T(8,128)} fusion(bf16[640,3200]{1,0:T(8,128)(2,1)S(1)} %copy-done.4, bf16[2048,640]{0,1:T(8,128)(2,1)S(1)} %copy-done.6, f32[2048]{0:T(1024)S(1)} %add_rsqrt_fusion), kind=kOutput, calls=%fused_computation.70 | convolution fusion | flops 8392540160 | bytes 32940032 | tf_op jit(solution)/shard_map/dot_general | solution.py:10
  504.6 36.0 %fusion.7 = (bf16[2048,3200]{0,1:T(8,128)(2,1)}, bf16[2048,3200]{0,1:T(8,128)(2,1)}, f32[2048,3200]{0,1:T(8,128)}) fusion(bf16[3200,2048]{1,0:T(8,128)(2,1)} %convolution_convert_fusion.1, f32[2048,3200]{0,1:T(8,128)} %fusion.54, bf16[640,3200]{1,0:T(8,128)(2,1)} %reshape.89, bf16[2048,640]{0,1:T(8,128)(2,1)S(1)} %copy-done.6, f32[2048]{0:T(1024)S(1)} %add_rsqrt_fusion), kind=kOutput, calls=%fused_computation.9 | convolution fusion | flops 8484290560 | bytes 98476032 | tf_op jit(solution)/shard_map/dot_general | solution.py:10
  540.6 13.3 %convolution_convert_fusion.8 = bf16[2048,640]{0,1:T(8,128)(2,1)S(1)} fusion(bf16[640,3200]{1,0:T(8,128)(2,1)} %reshape.89, bf16[2048,3200]{0,1:T(8,128)(2,1)} %get-tuple-element.27), kind=kOutput, calls=%fused_computation.57 | convolution fusion | flops 8389918720 | bytes 19824640 | tf_op jit(solution)/shard_map/dot_general | solution.py:10
  554.0 12.6 %fusion.21 = (f32[2048]{0:T(1024)S(1)}, bf16[2048,640]{0,1:T(8,128)(2,1)S(1)}) fusion(bf16[2048,640]{0,1:T(8,128)(2,1)S(1)} %copy-done.6, bf16[2048,640]{0,1:T(8,128)(2,1)S(1)} %convolution_convert_fusion.8, bf16[640,3200]{1,0:T(8,128)(2,1)S(1)} %copy-done.5, bf16[2048,3200]{0,1:T(8,128)(2,1)} %get-tuple-element.26), kind=kOutput, calls=%fused_computation.45 | convolution fusion | flops 8396470272 | bytes 25075712 | tf_op jit(solution)/shard_map/dot_general | solution.py:10
  570.0 33.3 %fusion.5 = (bf16[2048,3200]{0,1:T(8,128)(2,1)}, bf16[2048,3200]{0,1:T(8,128)(2,1)}) fusion(f32[2048,3200]{0,1:T(8,128)} %fusion.24, f32[2048,3200]{0,1:T(8,128)} %get-tuple-element.41, bf16[2048,640]{0,1:T(8,128)(2,1)} %fusion.43, bf16[1,3200,640]{2,1,0:T(8,128)(2,1)} %all-gather.14.cloned.1.call-done), kind=kOutput, calls=%fused_computation.5 | convolution fusion | flops 8486912000 | bytes 85360640 | tf_op jit(solution)/shard_map/dot_general | solution.py:10
  603.3 14.2 %convolution_convert_fusion.6 = bf16[640,3200]{1,0:T(8,128)(2,1)} fusion(bf16[2048,3200]{0,1:T(8,128)(2,1)} %get-tuple-element.25, bf16[1,2048,640]{1,2,0:T(8,128)(2,1)S(1)} %copy-done.1, f32[2048]{0:T(1024)S(1)} %copy-done.10), kind=kOutput, calls=%fused_computation.35 | convolution fusion | flops 8394588160 | bytes 19832832 | tf_op jit(solution)/shard_map/dot_general | solution.py:10
  617.5 24.8 %fusion.11 = bf16[3200,640]{1,0:T(8,128)(2,1)} fusion(f32[2048,3200]{0,1:T(8,128)} %get-tuple-element.44, f32[2048,3200]{0,1:T(8,128)} %fusion.54, bf16[1,2048,640]{2,1,0:T(8,128)(2,1)} %param.6), kind=kOutput, calls=%fused_computation.31 | convolution fusion | flops 8429977600 | bytes 59146240 | tf_op jit(solution)/shard_map/dot_general | solution.py:10
  649.2 15.6 %convolution_convert_fusion.4 = bf16[640,3200]{1,0:T(8,128)(2,1)} fusion(bf16[2048,3200]{0,1:T(8,128)(2,1)} %get-tuple-element.27, bf16[2048,640]{0,1:T(8,128)(2,1)} %get-tuple-element.43, f32[2048]{0:T(1024)S(1)} %add_rsqrt_fusion), kind=kOutput, calls=%fused_computation.33 | convolution fusion | flops 8394588160 | bytes 19832832 | tf_op jit(solution)/shard_map/dot_general | solution.py:10
  672.7 15.8 %convolution_convert_fusion.5 = bf16[640,3200]{1,0:T(8,128)(2,1)} fusion(bf16[2048,3200]{0,1:T(8,128)(2,1)} %get-tuple-element.26, bf16[2048,640]{0,1:T(8,128)(2,1)} %get-tuple-element.43, f32[2048]{0:T(1024)S(1)} %add_rsqrt_fusion), kind=kOutput, calls=%fused_computation.34 | convolution fusion | flops 8394588160 | bytes 19832832 | tf_op jit(solution)/shard_map/dot_general | solution.py:10
  696.4 12.3 %pad_maximum_fusion = bf16[4,4,8,375,128]{4,3,2,1,0:T(8,128)(2,1)} fusion(bf16[4,4,8,125,128]{4,3,2,1,0:T(8,128)(2,1)} %concatenate.16, bf16[4,4,8,125,128]{4,3,2,1,0:T(8,128)(2,1)} %concatenate.15, bf16[4,4,8,125,128]{4,3,2,1,0:T(8,128)(2,1)} %concatenate.14), kind=kLoop, calls=%fused_computation.19 | loop fusion | flops 36864000 | bytes 24576000 | tf_op jit(solution)/shard_map/concatenate | solution.py:63
  708.7 15.7 %convolution_convert_fusion.2 = bf16[3200,640]{1,0:T(8,128)(2,1)} fusion(bf16[2048,3200]{0,1:T(8,128)(2,1)} %get-tuple-element.40, bf16[2048,640]{0,1:T(8,128)(2,1)} %fusion.43), kind=kOutput, calls=%fused_computation.30 | convolution fusion | flops 8390656000 | bytes 19824640 | tf_op jit(solution)/shard_map/dot_general | solution.py:10
  725.3 97.0 %reduce-scatter.20.cloned.1.call-done = bf16[1,4,8,375,128]{4,3,2,1,0:T(8,128)(2,1)} async-done(((bf16[4,4,8,375,128]{4,3,2,1,0:T(8,128)(2,1)}), bf16[1,4,8,375,128]{4,3,2,1,0:T(8,128)(2,1)}) %reduce-scatter.20.cloned.1.call-update) | async-done | bytes 3072016 | tf_op jit(solution)/shard_map/reduce_scatter | solution.py:66
  822.3 14.4 %convolution_convert_fusion.3 = bf16[640,3200]{1,0:T(8,128)(2,1)} fusion(bf16[2048,3200]{0,1:T(8,128)(2,1)} %get-tuple-element.24, bf16[1,2048,640]{1,2,0:T(8,128)(2,1)S(1)} %copy-done.1, f32[2048]{0:T(1024)S(1)} %copy-done.10), kind=kOutput, calls=%fused_computation.32 | convolution fusion | flops 8394588160 | bytes 19832832 | tf_op jit(solution)/shard_map/dot_general | solution.py:10
  847.9 15.4 %fusion.32 = bf16[2048,640]{0,1:T(8,128)(2,1)} fusion(bf16[2048,3200]{0,1:T(8,128)(2,1)} %get-tuple-element.25, bf16[1,640,3200]{2,0,1:T(2,128)(2,1)} %all-gather.12.cloned.1.call-done), kind=kOutput, calls=%fused_computation.55 | convolution fusion | flops 8389918720 | bytes 19824640 | tf_op jit(solution)/shard_map/dot_general | solution.py:10
  863.3 9.9 reduce-scatter.24.cloned.1.call-done
  873.2 14.9 %fusion.18 = (f32[2048]{0:T(1024)S(1)}, bf16[2048,640]{0,1:T(8,128)(2,1)}) fusion(bf16[1,2048,640]{1,2,0:T(8,128)(2,1)S(1)} %copy-done.1, bf16[2048,640]{0,1:T(8,128)(2,1)} %fusion.32, bf16[640,3200]{1,0:T(8,128)(2,1)} %reshape.88, bf16[2048,3200]{0,1:T(8,128)(2,1)} %get-tuple-element.24), kind=kOutput, calls=%fused_computation.42 | convolution fusion | flops 8396470272 | bytes 25075712 | tf_op jit(solution)/shard_map/dot_general | solution.py:10
  888.1 14.9 %reduce-scatter.26.cloned.1.call-done = bf16[40,3200]{1,0:T(8,128)(2,1)} async-done(((bf16[160,3200]{1,0:T(8,128)(2,1)}), bf16[40,3200]{1,0:T(8,128)(2,1)}) %reduce-scatter.26.cloned.1.call-update) | async-done | bytes 256016
  903.0 42.6 %reduce-scatter.22.cloned.1.call-done = bf16[1,8,375,128]{3,2,1,0:T(8,128)(2,1)} async-done(((bf16[4,8,375,128]{3,2,1,0:T(8,128)(2,1)}), bf16[1,8,375,128]{3,2,1,0:T(8,128)(2,1)}) %reduce-scatter.22.cloned.1.call-update) | async-done | bytes 768016 | tf_op jit(solution)/shard_map/reduce_scatter | solution.py:66
  945.6 95.5 %reduce-scatter.28.cloned.1.call-done = bf16[1,1000,128]{2,1,0:T(8,128)(2,1)} async-done(((bf16[16,1000,128]{2,1,0:T(8,128)(2,1)}), bf16[1,1000,128]{2,1,0:T(8,128)(2,1)}) %reduce-scatter.28.cloned.1.call-update) | async-done | bytes 256016
  1041.2 29.5 %reduce-scatter.30.cloned.1.call-done = bf16[200,640]{1,0:T(8,128)(2,1)} async-done(((bf16[800,640]{1,0:T(8,128)(2,1)}), bf16[200,640]{1,0:T(8,128)(2,1)}) %reduce-scatter.30.cloned.1.call-update) | async-done | bytes 256016
  1070.6 22.2 %fusion.63 = (bf16[128,128]{1,0:T(8,128)(2,1)S(1)}, bf16[32,640]{1,0:T(8,128)(2,1)S(1)}) fusion(bf16[1000,128]{1,0:T(8,128)(2,1)} %bitcast.93, bf16[200,640]{1,0:T(8,128)(2,1)} %reduce-scatter.30.cloned.1.call-done), kind=kCustom, calls=%all-reduce-scatter.2 | all-reduce-scatter fusion | flops 294914 | bytes 586752
  1115.7 32.9 %all-reduce.13.cloned.1.call-done = (bf16[8,375,128]{2,1,0:T(8,128)(2,1)}, bf16[40,3200]{1,0:T(8,128)(2,1)}) async-done(((bf16[8,375,128]{2,1,0:T(8,128)(2,1)}, bf16[40,3200]{1,0:T(8,128)(2,1)}), (bf16[8,375,128]{2,1,0:T(8,128)(2,1)}, bf16[40,3200]{1,0:T(8,128)(2,1)})) %all-reduce.13.cloned.1.call-update) | async-done | bytes 1024016
  (102 shorter events, 112.0 us)
Async XLA Ops:
  7.2 123.7 %all-gather.18.cloned.1.call-start = ((), (), s32[]{:S(2)}) async-start(), calls=%async_computation.14 | async-start | bytes 4227072 | tf_op jit(solution)/shard_map/all_gather | solution.py:50
  9.1 246.8 %all-gather.12.cloned.1.call-start = ((), (), s32[]{:S(2)}) async-start(), calls=%async_computation.11 | async-start | bytes 8256000 | tf_op jit(solution)/shard_map/all_gather | solution.py:49
  10.9 294.2 %all-gather.14.cloned.1.call-start = ((), (), s32[]{:S(2)}) async-start(), calls=%async_computation.12 | async-start | bytes 5120000 | tf_op jit(solution)/shard_map/all_gather | solution.py:53
  55.5 387.4 %all-gather.16.cloned.1.call-start = ((), (), s32[]{:S(2)}) async-start(), calls=%async_computation.13 | async-start | bytes 12417024 | tf_op jit(solution)/shard_map/all_gather | solution.py:55
  56.4 668.1 %reduce-scatter.18.cloned.1.call-start = ((), (), s32[]{:S(2)}) async-start(), calls=%async_computation.7 | async-start | bytes 5120000 | tf_op jit(solution)/shard_map/reduce_scatter | solution.py:75
  59.5 245.6 %copy-start = (bf16[1,2048,640]{1,2,0:T(8,128)(2,1)}, bf16[1,2048,640]{1,2,0:T(8,128)(2,1)S(1)}, u32[]{:S(2)}) copy-start(bf16[1,2048,640]{1,2,0:T(8,128)(2,1)S(1)} %copy.49) | copy-start | bytes 7864324
  65.0 0.6 copy-start.7
  65.6 207.6 %copy-start.9 = (f32[2048]{0:T(1024)}, f32[2048]{0:T(1024)S(1)}, u32[]{:S(2)}) copy-start(f32[2048]{0:T(1024)S(1)} %add_rsqrt_fusion.1) | copy-start | bytes 24580
  255.9 17.3 %copy-start.3 = (bf16[640,3200]{1,0:T(8,128)(2,1)S(1)}, bf16[640,3200]{1,0:T(8,128)(2,1)}, u32[]{:S(2)}) copy-start(bf16[640,3200]{1,0:T(8,128)(2,1)} %reshape.88) | copy-start | bytes 12288004
  474.1 16.7 %copy-start.4 = (bf16[640,3200]{1,0:T(8,128)(2,1)S(1)}, bf16[640,3200]{1,0:T(8,128)(2,1)}, u32[]{:S(2)}) copy-start(bf16[640,3200]{1,0:T(8,128)(2,1)} %reshape.90) | copy-start | bytes 12288004
  474.1 16.7 %copy-start.6 = (bf16[2048,640]{0,1:T(8,128)(2,1)S(1)}, bf16[2048,640]{0,1:T(8,128)(2,1)}, u32[]{:S(2)}) copy-start(bf16[2048,640]{0,1:T(8,128)(2,1)} %get-tuple-element.43) | copy-start | bytes 7864324
  540.6 13.3 %copy-start.5 = (bf16[640,3200]{1,0:T(8,128)(2,1)S(1)}, bf16[640,3200]{1,0:T(8,128)(2,1)}, u32[]{:S(2)}) copy-start(bf16[640,3200]{1,0:T(8,128)(2,1)} %reshape.90) | copy-start | bytes 12288004
  554.0 12.7 %copy-start.2 = (bf16[1,2048,640]{1,2,0:T(8,128)(2,1)S(1)}, bf16[1,2048,640]{1,2,0:T(8,128)(2,1)}, u32[]{:S(2)}) copy-start(bf16[1,2048,640]{1,2,0:T(8,128)(2,1)} %copy.48) | copy-start | bytes 7864324
  570.0 33.3 %copy-start.1 = (bf16[1,2048,640]{1,2,0:T(8,128)(2,1)S(1)}, bf16[1,2048,640]{1,2,0:T(8,128)(2,1)}, u32[]{:S(2)}) copy-start(bf16[1,2048,640]{1,2,0:T(8,128)(2,1)} %copy-done) | copy-start | bytes 7864324
  570.0 33.3 %copy-start.10 = (f32[2048]{0:T(1024)S(1)}, f32[2048]{0:T(1024)}, u32[]{:S(2)}) copy-start(f32[2048]{0:T(1024)} %copy-done.9) | copy-start | bytes 24580
  617.5 204.7 %reduce-scatter.20.cloned.1.call-start = ((), (), s32[]{:S(2)}) async-start(), calls=%async_computation.8 | async-start | bytes 15400960 | tf_op jit(solution)/shard_map/reduce_scatter | solution.py:66
  708.7 164.5 %reduce-scatter.24.cloned.1.call-start = ((), (), s32[]{:S(2)}) async-start(), calls=%async_computation.10 | async-start | bytes 5120000 | tf_op jit(solution)/shard_map/reduce_scatter | solution.py:70
  724.5 178.5 %reduce-scatter.26.cloned.1.call-start = ((), (), s32[]{:S(2)}) async-start(), calls=%async_computation.15 | async-start | bytes 1280000
  725.2 220.4 %reduce-scatter.22.cloned.1.call-start = ((), (), s32[]{:S(2)}) async-start(), calls=%async_computation.9 | async-start | bytes 3850240 | tf_op jit(solution)/shard_map/reduce_scatter | solution.py:66
  822.2 218.9 %reduce-scatter.28.cloned.1.call-start = ((), (), s32[]{:S(2)}) async-start(), calls=%async_computation.16 | async-start | bytes 4352000
  836.7 8.7 copy-start.11
  845.3 225.4 %reduce-scatter.30.cloned.1.call-start = ((), (), s32[]{:S(2)}) async-start(), calls=%async_computation.17 | async-start | bytes 1280000
  873.2 14.9 %copy-start.8 = (f32[2048]{0:T(1024)S(1)}, f32[2048]{0:T(1024)}, u32[]{:S(2)}) copy-start(f32[2048]{0:T(1024)} %copy-done.7) | copy-start | bytes 24580
  873.2 275.4 %all-reduce.13.cloned.1.call-start = ((), (), s32[]{:S(2)}) async-start(), calls=%async_computation.18 | async-start | bytes 2052096
  1092.9 20.7 %collective-permute-start = (bf16[21,128]{1,0:T(8,128)(2,1)S(1)}, bf16[21,128]{1,0:T(8,128)(2,1)S(1)}, u32[]{:S(2)}, u32[]{:S(2)}) collective-permute-start(bf16[21,128]{1,0:T(8,128)(2,1)S(1)} %slice.54), channel_id=1, source_target_pairs={{0,1},{1,2},{2,3},{3,4},{4,5},{5,6},{6,7},{8,9},{9,10},{10,11},{11... | collective-permute-start | bytes 16136
  1105.3 9.8 collective-permute-start.1
  1108.5 6.6 collective-permute-start.2
Sparse Core Ops, SparseCore 0:
  12.2 118.6 all-gather.17
  135.0 120.8 all-gather.11
  257.7 47.2 all-gather.13
  308.6 134.2 all-gather.15
  617.6 46.9 reduce-scatter.17
  708.8 113.3 reduce-scatter.19
  824.8 48.3 reduce-scatter.23
  875.7 27.1 reduce-scatter.25
  905.6 40.0 reduce-scatter.21
  949.3 91.8 reduce-scatter.27
  1043.7 26.8 reduce-scatter.29
  1072.9 75.6 all-reduce.12

commit v2 on v1

v2 whole, which is shorter than its diff:
```python
import functools

import jax
import jax.numpy as jnp
from jax import lax
from jax.experimental import pallas as pl
from jax.experimental.pallas import tpu as pltpu
from jax.sharding import PartitionSpec as P

F32, BF16 = jnp.float32, jnp.bfloat16
MESH = pl.DeviceIdType.MESH
SIDE = 4
VMEM = pltpu.VMEM
DMA = pltpu.SemaphoreType.DMA


def place(depth):
    me = lax.axis_index("dp")
    z = lax.rem(me, depth)
    y = lax.rem(me // depth, SIDE)
    x = me // (depth * SIDE)
    return lax.axis_index("rep"), x, y, z, lambda x, y, z: (x * SIDE + y) * depth + z


def turn(i, by, n):
    return lax.rem(i + by + n, n)


def meet(peers):
    barrier = pltpu.get_barrier_semaphore()
    for peer in peers:
        pl.semaphore_signal(barrier, inc=1, device_id=peer, device_id_type=MESH)
    pl.semaphore_wait(barrier, len(peers))


class Copies:
    def __init__(self, send, recv):
        self.send, self.recv, self.used, self.open = send, recv, 0, []

    def make(self, src, dst, peer):
        k = self.used
        self.used += 1
        return pltpu.make_async_remote_copy(src, dst, self.send.at[k], self.recv.at[k], device_id=peer, device_id_type=MESH)

    def start(self, src, dst, peer):
        copy = self.make(src, dst, peer)
        copy.start()
        self.open.append(copy)
        return copy

    def drain(self):
        for copy in self.open:
            copy.wait_send()
        self.open = []


def z_gather_kernel(depth, parts, own, out, send, recv, local):
    core, x, y, z, index = place(depth)
    right, left = ({"dp": index(x, y, turn(z, by, depth))} for by in (1, -1))
    partner = {"rep": 1 - core}
    half = parts // 2
    fill = pltpu.make_async_copy(own, out.at[z], local)
    fill.start()
    meet((right, left, partner))
    copies = Copies(send, recv)

    def block(by, j):
        return out.at[turn(z, by, depth), core * half + j]

    fill.wait()
    from_left, from_right, relays = {}, {}, []
    steps = depth // 2
    for s in range(steps + 1):
        for j in range(half):
            if s:
                from_left[s - 1, j].wait_recv()
                relays.append(copies.start(block(-s, j), block(-s, j), partner))
            if s < steps:
                from_left[s, j] = copies.start(block(-s, j), block(-s, j), right)
            if 0 < s < depth - steps:
                from_right[s - 1, j].wait_recv()
                relays.append(copies.start(block(s, j), block(s, j), partner))
            if s < depth - 1 - steps:
                from_right[s, j] = copies.start(block(s, j), block(s, j), left)
    for relay in relays:
        relay.wait_recv()
    copies.drain()


def z_gather(own, depth, cid):
    parts = own.shape[0]
    count = parts // 2 * (depth - 1) * 2
    return pl.pallas_call(
        functools.partial(z_gather_kernel, depth, parts),
        out_shape=jax.ShapeDtypeStruct((depth, *own.shape), own.dtype),
        in_specs=[pl.BlockSpec(memory_space=pl.ANY)],
        out_specs=pl.BlockSpec(memory_space=VMEM),
        scratch_shapes=[DMA((count,)), DMA((count,)), DMA],
        compiler_params=pltpu.CompilerParams(collective_id=cid, has_side_effects=True),
        name="z_gather",
    )(own)


def columns(n):
    cut = -(-n // 256) * 128
    return pl.ds(0, cut), pl.ds(cut, n - cut)


def cut_rows(ref):
    lead = ref.shape[0]
    cut = 2 if len(ref.shape) == 3 else -(-lead // 16) * 8
    return ref.at[pl.ds(0, cut)], ref.at[pl.ds(cut, lead - cut)]


def gather_half(copies, region, pos, right, left, partner):
    own, before, after, far = (region(turn(pos, by, SIDE)) for by in (0, -1, 1, 2))
    to_right = copies.start(own, own, right)
    to_left = copies.start(own, own, left)
    yield
    to_right.wait_recv()
    first, second = cut_rows(before)[0], cut_rows(after)[1]
    go = copies.start(first, first, right)
    to_left.wait_recv()
    back = copies.start(second, second, left)
    relays = [copies.start(before, before, partner), copies.start(after, after, partner)]
    yield
    go.wait_recv()
    back.wait_recv()
    relays.append(copies.start(far, far, partner))
    return relays


def gather_job(copies, ref, core_ring, which):
    x, y, xr, xl, yr, yl, partner = core_ring
    cols = columns(ref.shape[-1])[which]
    one = lambda i, j: ref.at[i, j, :, cols]
    if which == 0:
        relays = yield from gather_half(copies, lambda i: one(x, i), y, yr, yl, partner)
        relays += yield from gather_half(copies, lambda i: ref.at[i, :, :, cols], x, xr, xl, partner)
    else:
        relays = yield from gather_half(copies, lambda i: one(i, y), x, xr, xl, partner)
        relays += yield from gather_half(copies, lambda i: ref.at[:, i, :, cols], y, yr, yl, partner)
    return relays


GATHER_COPIES = 2 * (4 + 3)


def neighbours(depth):
    core, x, y, z, index = place(depth)
    xr, xl = ({"dp": index(turn(x, by, SIDE), y, z)} for by in (1, -1))
    yr, yl = ({"dp": index(x, turn(y, by, SIDE), z)} for by in (1, -1))
    return core, (x, y, xr, xl, yr, yl, {"rep": 1 - core})


def run_together(jobs):
    done = [None] * len(jobs)
    live = list(range(len(jobs)))
    while live:
        for k in list(live):
            try:
                next(jobs[k])
            except StopIteration as stop:
                done[k] = stop.value
                live.remove(k)
    return done


def xy_gather_kernel(depth, own0, own1, own2, out0, out1, out2, send, recv, local):
    core, ring = neighbours(depth)
    x, y = ring[:2]
    fills = []
    for own, out in ((own0, out0), (own1, out1), (own2, out2)):
        for k in range(2):
            fills.append(pltpu.make_async_copy(own.at[k], out.at[k, x, y], local.at[len(fills)]))
            fills[-1].start()
    meet(ring[2:])
    for fill in fills:
        fill.wait()
    copies = Copies(send, recv)
    jobs = [gather_job(copies, out.at[core], ring, which) for out in (out0, out2, out1) for which in range(2)]
    for relays in run_together(jobs):
        for relay in relays:
            relay.wait_recv()
    copies.drain()


def xy_gather(own0, own1, own2, depth, cid):
    owns = (own0, own1, own2)
    count = 6 * GATHER_COPIES
    return pl.pallas_call(
        functools.partial(xy_gather_kernel, depth),
        out_shape=[jax.ShapeDtypeStruct((2, SIDE, SIDE, *own.shape[1:]), own.dtype) for own in owns],
        in_specs=[pl.BlockSpec(memory_space=pl.ANY)] * 3,
        out_specs=[pl.BlockSpec(memory_space=pl.ANY)] * 3,
        scratch_shapes=[DMA((count,)), DMA((count,)), DMA((6,))],
        compiler_params=pltpu.CompilerParams(collective_id=cid, has_side_effects=True),
        name="xy_gather",
    )(*owns)


def each_block(fn, lead):
    if lead is None:
        fn(())
    else:
        pl.loop(0, lead)(lambda i: fn((i,)))


def add_up(dst, parts):
    lead = dst.shape[0] if len(dst.shape) == 3 else None

    def block(at):
        total = parts[0][at].astype(F32) if at else parts[0][...].astype(F32)
        for part in parts[1:]:
            total += (part[at] if at else part[...]).astype(F32)
        if at:
            dst[at] = total.astype(dst.dtype)
        else:
            dst[...] = total.astype(dst.dtype)

    each_block(block, lead)


def scatter_half(copies, term, exact, buffers, pos, right, left, dst):
    far_l, far_r, near_l, near_r, out_l, out_r = buffers
    ahead, behind = turn(pos, 1, SIDE), turn(pos, -1, SIDE)
    far0, far1 = cut_rows(term(turn(pos, 2, SIDE)))
    after0, before1 = cut_rows(term(ahead))[0], cut_rows(term(behind))[1]
    (nl0, nl1), (nr0, nr1) = map(cut_rows, (near_l, near_r))
    to_left = copies.start(far0, far_r, left)
    to_right = copies.start(far1, far_l, right)
    plain = [copies.start(after0, nl0, right), copies.start(before1, nr1, left)]
    yield
    to_left.wait_recv()
    add_up(out_l, (cut_rows(exact(behind))[0], far_r))
    plain.append(copies.start(out_l, nr0, left))
    to_right.wait_recv()
    add_up(out_r, (cut_rows(exact(ahead))[1], far_l))
    plain.append(copies.start(out_r, nl1, right))
    yield
    for copy in plain:
        copy.wait_recv()
    add_up(dst, (exact(pos), near_l, near_r))


SCATTER_COPIES = 2 * 6


def scatter_job(copies, ref, order, ring, first, total, cast, second, out):
    x, y, xr, xl, yr, yl = ring
    along_x, along_y = (x, xr, xl), (y, yr, yl)
    if order == 0:
        one, two, term = along_x, along_y, lambda i: ref.at[i]
    else:
        one, two, term = along_y, along_x, lambda i: ref.at[:, i]
    yield from scatter_half(copies, term, term, first, *one, total)

    @pl.loop(0, SIDE)
    def _(i):
        cast[i] = total[i].astype(BF16)

    yield from scatter_half(copies, lambda i: cast.at[i], lambda i: total.at[i], second, *two, out)


def scatter_scratch(rows, cols):
    cut = -(-rows // 16) * 8
    half, whole = VMEM((2, rows, cols), BF16), VMEM((SIDE, rows, cols), BF16)
    near, top, low = VMEM((rows, cols), BF16), VMEM((cut, cols), BF16), VMEM((rows - cut, cols), BF16)
    first = [half, half, whole, whole, half, half]
    second = [low, top, near, near, top, low]
    return [*first, VMEM((SIDE, rows, cols), F32), whole, *second]


def xy_scatter_kernel(depth, *refs):
    ins, outs, (send, recv), scratch = refs[:3], refs[3:6], refs[6:8], refs[8:]
    _, ring = neighbours(depth)
    meet(ring[2:-1])
    copies = Copies(send, recv)
    jobs = []
    for ref, out in zip(ins, outs):
        for which in range(2):
            mine, scratch = scratch[:14], scratch[14:]
            cols = columns(ref.shape[-1])[which]
            jobs.append(scatter_job(copies, ref.at[:, :, :, cols], which, ring[:-1], mine[:6], mine[6], mine[7], mine[8:], out.at[:, cols]))
    run_together(jobs)
    copies.drain()


def xy_scatter(terms, depth, cid):
    scratch = [DMA((6 * SCATTER_COPIES,)), DMA((6 * SCATTER_COPIES,))]
    for term in terms:
        scratch += [spec for cols in columns(term.shape[-1]) for spec in scatter_scratch(term.shape[2], cols.size)]
    return pl.pallas_call(
        functools.partial(xy_scatter_kernel, depth),
        out_shape=[jax.ShapeDtypeStruct(term.shape[2:], F32) for term in terms],
        in_specs=[pl.BlockSpec(memory_space=VMEM)] * 3,
        out_specs=[pl.BlockSpec(memory_space=VMEM)] * 3,
        scratch_shapes=scratch,
        compiler_params=pltpu.CompilerParams(collective_id=cid, has_side_effects=True, vmem_limit_bytes=60 << 20),
        name="xy_scatter",
    )(*terms)


def z_scatter_kernel(depth, parts, own, out, in_r, out_r, in_l, out_l, send, recv):
    _, x, y, z, index = place(depth)
    right, left = ({"dp": index(x, y, turn(z, by, depth))} for by in (1, -1))
    meet((right, left))
    copies = Copies(send, recv)
    n_right = depth // 2
    n_left = depth - 1 - n_right
    going = {}
    for s in range(n_right):
        for j in range(parts):
            for way, steps, inbox, outbox, peer in ((1, n_right, in_r, out_r, right), (-1, n_left, in_l, out_l, left)):
                if s >= steps:
                    continue
                value = own[turn(z, way * (steps - s), depth), j]
                if s:
                    going[way, s - 1, j].wait_recv()
                    value += inbox[s - 1, j].astype(F32)
                outbox[s, j] = value.astype(BF16)
                going[way, s, j] = copies.start(outbox.at[s, j], inbox.at[s, j], peer)
    for j in range(parts):
        value = own[z, j]
        for way, steps, inbox in ((1, n_right, in_r), (-1, n_left, in_l)):
            if steps:
                going[way, steps - 1, j].wait_recv()
                value += inbox[steps - 1, j].astype(F32)
        out[j] = value.astype(BF16)
    copies.drain()


def z_scatter(own, cid):
    depth, parts, rows, lanes = own.shape
    boxes = [VMEM((max(steps, 1), parts, rows, lanes), BF16) for steps in (depth // 2, depth // 2, depth - 1 - depth // 2, depth - 1 - depth // 2)]
    count = parts * (depth - 1)
    return pl.pallas_call(
        functools.partial(z_scatter_kernel, depth, parts),
        out_shape=jax.ShapeDtypeStruct(own.shape[1:], BF16),
        in_specs=[pl.BlockSpec(memory_space=VMEM)],
        out_specs=pl.BlockSpec(memory_space=VMEM),
        scratch_shapes=[*boxes, DMA((count,)), DMA((count,))],
        compiler_params=pltpu.CompilerParams(collective_id=cid, has_side_effects=True),
        name="z_scatter",
    )(own)


def flat(t):
    t = t.reshape(-1, 128)
    return jnp.pad(t, ((0, -t.shape[0] % 8), (0, 0)))


def unflat(t, shape):
    size = 1
    for n in shape:
        size *= n
    return t[..., : size // 128, :].reshape(*t.shape[:-2], *shape)


def gather_weights(wg, wu, wd, depth):
    own = jnp.stack([flat(t) for t in (wg[0], wg[1], wd[0], wu[0], wu[1], wd[1])])
    got = z_gather(own, depth, 1)
    g0, g1, d0, u0, u1, d1 = (unflat(got[:, k], t.shape[1:]).reshape(-1, t.shape[2]) for k, t in enumerate((wg, wg, wd, wu, wu, wd)))
    return xy_gather(jnp.stack([g0, u0]), jnp.stack([g1, u1]), jnp.stack([d0, d1]), depth, 2)


def scatter_grads(sums, shapes, depth):
    own = []
    for t, shape in zip(sums, shapes):
        t = t.reshape(depth, -1, 128)
        own.append(jnp.pad(t, ((0, 0), (0, -t.shape[1] % 8), (0, 0))))
    out = z_scatter(jnp.stack(own, 1), 5)
    return [unflat(out[k], shape) for k, shape in enumerate(shapes)]


def dot(a, b, ca, cb):
    return lax.dot_general(a, b, (((ca,), (cb,)), ((), ())), preferred_element_type=F32)


def norm_parts(h):
    wide = h.astype(F32)
    scale = lax.rsqrt(jnp.mean(wide**2, -1, keepdims=True) + 1e-6)
    return wide, scale


def forward(h, wg, wu, wd, last):
    wide, scale = norm_parts(h)
    a = (wide * scale).astype(BF16)
    gate, up = dot(a, wg, 1, 0), dot(a, wu, 1, 0)
    p = (jax.nn.silu(gate) * up).astype(BF16)
    out = None if last else h + dot(p, wd, 1, 0).astype(BF16)
    return out, (wide, scale, a, gate, up, p)


def backward(d, saved, wg, wu, wd):
    wide, scale, a, gate, up, p = saved
    dp = dot(d, wd, 1, 1).astype(BF16).astype(F32)
    dwd = dot(p, d, 0, 0).astype(BF16)
    sig = jax.nn.sigmoid(gate)
    dg = (dp * up * (sig * (1 + gate * (1 - sig)))).astype(BF16)
    du = (dp * gate * sig).astype(BF16)
    dwg, dwu = dot(a, dg, 0, 0).astype(BF16), dot(a, du, 0, 0).astype(BF16)
    da = (dot(dg, wg, 1, 1).astype(BF16) + dot(du, wu, 1, 1).astype(BF16)).astype(F32)
    inner = jnp.sum(da * wide, -1, keepdims=True) / wide.shape[-1]
    dwide = da * scale - wide * (scale**3 * inner)
    return d + dwide.astype(BF16), dwg, dwu, dwd


def solution(mesh):
    n = mesh.shape["dp"]
    depth = n // SIDE**2

    def step(x, dy, wg, wu, wd):
        d_model, ff = wg.shape[1] * n, wg.shape[2]
        gu0, gu1, down = gather_weights(wg, wu, wd, depth)
        wg0, wu0, wg1, wu1 = (t.reshape(d_model, ff) for t in (*gu0, *gu1))
        wd0, wd1 = (t.reshape(ff, d_model) for t in down)
        h1, saved0 = forward(x[0], wg0, wu0, wd0, False)
        _, saved1 = forward(h1, wg1, wu1, wd1, True)
        dh, *terms1 = backward(dy[0], saved1, wg1, wu1, wd1)
        dh, *terms0 = backward(dh, saved0, wg0, wu0, wd0)
        sums = []
        for k, terms in enumerate((terms0, terms1)):
            sums += xy_scatter([t.reshape(SIDE, SIDE, -1, t.shape[1]) for t in terms], depth, 3 + k)
        g0, u0, d0, g1, u1, d1 = scatter_grads(sums, [t.shape[1:] for t in (wg, wu, wd)] * 2, depth)
        return dh[None], jnp.stack([g0, g1]), jnp.stack([u0, u1]), jnp.stack([d0, d1])

    data = P(("rep", "dp"), None, None)
    weight = P(None, "dp", None)
    grad = P("rep", "dp", None)
    return jax.shard_map(step, mesh=mesh, in_specs=(data, data, weight, weight, weight), out_specs=(data, grad, grad, grad), check_vma=False)
```

time: 1170 us -> 706 us (0.60)
  waiting for transfers between devices: 634 us -> 0 us
  Pallas kernels: 0 us -> 322 us
  blocking collectives: 65.6 us -> 0 us
  local copies, waits for them, and re-layouts: 93.9 us -> 54.7 us
  between operations: 16.9 us -> 1.28 us
    pallas_call x0 -> x5, Pallas kernels: none -> 322 us  [the longest x2 152 us: xy_scatter(): pl.pallas_call(functools.partial(xy_scatter_kernel, depth), out_shape=[ja...]
    all_gather x4 -> x0, waiting for transfers between devices: 309 us -> none  [the longest x1 123 us: step(): flat = lax.all_gather(flat, every, axis=0)]
    unnamed x19 -> x0, waiting for transfers between devices: 175 us -> none
    reduce_scatter x4 -> x0, waiting for transfers between devices: 149 us -> none  [the longest x2 140 us: step(): flat = lax.psum_scatter(flat, axis, scatter_dimension=0)]
    all_gather x2 -> x0, blocking collectives: 43.4 us -> none  [step(): wd0 = lax.all_gather(wd0, axis, axis=0, tiled=True)]
    reshape x5 -> x6, local copies, waits for them, and re-layouts: 38.2 us -> 9.97 us  [scatter_grads(): t = t.reshape(depth, -1, 128)]
    concatenate x3 -> x0, local copies, waits for them, and re-layouts: 22.5 us -> none  [step(): flat = jnp.concatenate([t.reshape(n, -1, 128) for t in (g1, u1, d1)], 1)]
    unnamed x1 -> x0, blocking collectives: 22.2 us -> none
  transfers between devices with their start and end apart: 15 -> 0, of which waited for: 12 -> 0; matrix products, arithmetic and copies ran while one was open for 24% -> 0% of each run, Pallas kernels for 0% -> 0%
where the time goes in v2:
time: 706 us; the launch traced here: 700 us
  Pallas kernels  322 us (46%)
  matrix products  309 us (44%)
  local copies, waits for them, and re-layouts  54.7 us (8%)
  other arithmetic  13.1 us (2%)
    dot_general x17, matrix products, dot(): lax.dot_general(a, b, (((ca,), (cb,)), ((), ())), preferred_element_type=...  309 us
    pallas_call x2, Pallas kernels, xy_scatter(): pl.pallas_call(functools.partial(xy_scatter_kernel, depth), out_shape=[ja...  152 us
    pallas_call x1, Pallas kernels, xy_gather(): pl.pallas_call(functools.partial(xy_gather_kernel, depth), out_shape=[jax...  124 us
    pallas_call x1, Pallas kernels, z_scatter(): pl.pallas_call(functools.partial(z_scatter_kernel, depth, parts), out_sha...  23.7 us
    pallas_call x1, Pallas kernels, z_gather(): pl.pallas_call(functools.partial(z_gather_kernel, depth, parts), out_shap...  21.7 us
    unnamed x51, local copies, waits for them, and re-layouts  19.4 us

profile of v2, /device:TPU:32, one launch (start us, length us, event | category | flops | bytes accessed | tf_op | source)
XLA Modules:
  0.0 700.2 jit_solution(17747196739600007187)
XLA Ops:
  5.4 21.7 %z_gather.1 = bf16[8,6,128,128]{3,2,1,0:T(8,128)(2,1)} custom-call(bf16[6,128,128]{2,1,0:T(8,128)(2,1)} %copy-done.12), custom_call_target="tpu_custom_call" | custom-call | tf_op jit(solution)/shard_map/z_gather/pallas_call | solution.py:93
  32.8 124.1 %xy_gather.1 = (bf16[2,4,4,40,3200]{4,3,2,1,0:T(8,128)(2,1)}, bf16[2,4,4,40,3200]{4,3,2,1,0:T(8,128)(2,1)}, bf16[2,4,4,200,640]{4,3,2,1,0:T(8,128)(2,1)}) custom-call(bf16[2,40,3200]{2,1,0:T(8,128)(2,1)} %pad_maximum_fusion.own0, bf16[2,40,3200]{2,1,0:T(8,128)(2,1)} %pad_maximum_fusion.1.own1, bf16[2,200,640]{2,1,0:T(8,128)(2,1)} %pad_maximum_fusion.2.own2), custom_call_target="tpu_custom_call" | custom-call | tf_op jit(solution)/shard_map/xy_gather/pallas_call | solution.py:191
  156.9 12.3 %fusion.45 = (bf16[1,4,4,40,3200]{4,3,2,1,0:T(8,128)(2,1)}, bf16[1,4,4,40,3200]{4,3,2,1,0:T(8,128)(2,1)}, bf16[1,4,4,40,3200]{4,3,2,1,0:T(8,128)(2,1)}, bf16[1,4,4,40,3200]{4,3,2,1,0:T(8,128)(2,1)}) fusion(bf16[2,4,4,40,3200]{4,3,2,1,0:T(8,128)(2,1)} %get-tuple-element.15, bf16[2,4,4,40,3200]{4,3,2,1,0:T(8,128)(2,1)} %get-tuple-element.14), kind=kLoop, calls=%fused_computation.102 | loop fusion | bytes 32768000 | tf_op jit(solution)/shard_map/unstack | solution.py:416
  169.3 3.0 copy.32
  173.8 18.1 %fusion.39 = f32[2048,3200]{0,1:T(8,128)} fusion(bf16[640,3200]{1,0:T(8,128)(2,1)} %bitcast.112, bf16[1,2048,640]{2,1,0:T(8,128)(2,1)} %param.5, f32[2048]{0:T(1024)S(1)} %add_rsqrt_fusion.1), kind=kOutput, calls=%fused_computation.63 | convolution fusion | flops 8392540160 | bytes 32940032 | tf_op jit(solution)/shard_map/dot_general | solution.py:377
  191.9 28.0 %multiply_convert_fusion.1 = (bf16[2048,3200]{0,1:T(8,128)(2,1)}, f32[2048,3200]{0,1:T(8,128)}) fusion(f32[2048,3200]{0,1:T(8,128)} %fusion.39, bf16[640,3200]{1,0:T(8,128)(2,1)S(1)} %bitcast.115, bf16[1,2048,640]{2,1,0:T(8,128)(2,1)} %param.5, f32[2048]{0:T(1024)S(1)} %add_rsqrt_fusion.1), kind=kOutput, calls=%fused_computation.14 | convolution fusion | flops 8431861760 | bytes 72261632 | tf_op jit(solution)/shard_map/dot_general | solution.py:377
  220.0 3.8 fusion.44
  223.8 14.5 %fusion.17 = (f32[2048]{0:T(1024)S(1)}, bf16[2048,640]{0,1:T(8,128)(2,1)S(1)}) fusion(bf16[2048,3200]{0,1:T(8,128)(2,1)} %get-tuple-element.58, bf16[3200,640]{1,0:T(8,128)(2,1)S(1)} %bitcast.126, bf16[1,2048,640]{1,2,0:T(8,128)(2,1)S(1)} %copy.32), kind=kOutput, calls=%fused_computation.42 | convolution fusion | flops 8395159552 | bytes 22454272 | tf_op jit(solution)/shard_map/dot_general | solution.py:377
  238.3 14.0 %fusion.33 = f32[2048,3200]{0,1:T(8,128)} fusion(bf16[640,3200]{1,0:T(8,128)(2,1)S(1)} %bitcast.116, bf16[2048,640]{0,1:T(8,128)(2,1)S(1)} %get-tuple-element.61, f32[2048]{0:T(1024)S(1)} %add_rsqrt_fusion), kind=kOutput, calls=%fused_computation.60 | convolution fusion | flops 8392540160 | bytes 32940032 | tf_op jit(solution)/shard_map/dot_general | solution.py:377
  252.3 14.9 %convolution_convert_fusion.1 = bf16[3200,2048]{1,0:T(8,128)(2,1)} fusion(bf16[3200,640]{1,0:T(8,128)(2,1)S(1)} %bitcast.128, bf16[1,2048,640]{2,1,0:T(8,128)(2,1)} %param.6), kind=kOutput, calls=%fused_computation.17 | convolution fusion | flops 8395161600 | bytes 19824640 | tf_op jit(solution)/shard_map/dot_general | solution.py:377
  267.2 36.5 %fusion.5 = (bf16[2048,3200]{0,1:T(8,128)(2,1)}, bf16[2048,3200]{0,1:T(8,128)(2,1)}, f32[2048,3200]{0,1:T(8,128)}) fusion(bf16[3200,2048]{1,0:T(8,128)(2,1)} %convolution_convert_fusion.1, f32[2048,3200]{0,1:T(8,128)} %fusion.33, bf16[640,3200]{1,0:T(8,128)(2,1)} %bitcast.118, bf16[2048,640]{0,1:T(8,128)(2,1)S(1)} %copy-done.10, f32[2048]{0:T(1024)S(1)} %add_rsqrt_fusion), kind=kOutput, calls=%fused_computation.9 | convolution fusion | flops 8484290560 | bytes 98476032 | tf_op jit(solution)/shard_map/dot_general | solution.py:377
  303.7 24.3 %fusion.9 = bf16[3200,640]{1,0:T(8,128)(2,1)} fusion(f32[2048,3200]{0,1:T(8,128)} %get-tuple-element.62, f32[2048,3200]{0,1:T(8,128)} %fusion.33, bf16[1,2048,640]{2,1,0:T(8,128)(2,1)} %param.6), kind=kOutput, calls=%fused_computation.30 | convolution fusion | flops 8429977600 | bytes 59146240 | tf_op jit(solution)/shard_map/dot_general | solution.py:377
  328.0 14.3 %convolution_convert_fusion.3 = bf16[640,3200]{1,0:T(8,128)(2,1)} fusion(bf16[2048,3200]{0,1:T(8,128)(2,1)} %get-tuple-element.39, bf16[2048,640]{0,1:T(8,128)(2,1)S(1)} %copy-done.10, f32[2048]{0:T(1024)S(1)} %add_rsqrt_fusion), kind=kOutput, calls=%fused_computation.31 | convolution fusion | flops 8394588160 | bytes 19832832 | tf_op jit(solution)/shard_map/dot_general | solution.py:377
  342.3 14.2 %convolution_convert_fusion.4 = bf16[640,3200]{1,0:T(8,128)(2,1)} fusion(bf16[2048,3200]{0,1:T(8,128)(2,1)} %get-tuple-element.38, bf16[2048,640]{0,1:T(8,128)(2,1)S(1)} %copy-done.10, f32[2048]{0:T(1024)S(1)} %add_rsqrt_fusion), kind=kOutput, calls=%fused_computation.32 | convolution fusion | flops 8394588160 | bytes 19832832 | tf_op jit(solution)/shard_map/dot_general | solution.py:377
  356.5 76.0 %xy_scatter.3 = (f32[40,3200]{1,0:T(8,128)}, f32[40,3200]{1,0:T(8,128)}, f32[200,640]{1,0:T(8,128)}) custom-call(bf16[4,4,40,3200]{3,2,1,0:T(8,128)(2,1)} %bitcast.124, bf16[4,4,40,3200]{3,2,1,0:T(8,128)(2,1)} %bitcast.122, bf16[4,4,200,640]{3,2,1,0:T(8,128)(2,1)} %bitcast.121), custom_call_target="tpu_custom_call" | custom-call | tf_op jit(solution)/shard_map/xy_scatter/pallas_call | solution.py:293
  432.5 1.9 reshape.121
  434.5 13.5 %convolution_convert_fusion.9 = bf16[2048,640]{0,1:T(8,128)(2,1)S(1)} fusion(bf16[640,3200]{1,0:T(8,128)(2,1)} %bitcast.119, bf16[2048,3200]{0,1:T(8,128)(2,1)} %get-tuple-element.39), kind=kOutput, calls=%fused_computation.48 | convolution fusion | flops 8389918720 | bytes 19824640 | tf_op jit(solution)/shard_map/dot_general | solution.py:377
  448.0 13.3 %fusion.19 = (f32[2048]{0:T(1024)S(1)}, bf16[2048,640]{0,1:T(8,128)(2,1)}) fusion(bf16[2048,640]{0,1:T(8,128)(2,1)S(1)} %copy-done.10, bf16[2048,640]{0,1:T(8,128)(2,1)S(1)} %convolution_convert_fusion.9, bf16[640,3200]{1,0:T(8,128)(2,1)S(1)} %bitcast.117, bf16[2048,3200]{0,1:T(8,128)(2,1)} %get-tuple-element.38), kind=kOutput, calls=%fused_computation.44 | convolution fusion | flops 8396470272 | bytes 25075712 | tf_op jit(solution)/shard_map/dot_general | solution.py:377
  461.4 3.0 copy.31
  464.4 4.3 fusion.24
  468.7 15.8 %convolution_convert_fusion.2 = bf16[3200,640]{1,0:T(8,128)(2,1)} fusion(bf16[2048,3200]{0,1:T(8,128)(2,1)} %get-tuple-element.58, bf16[2048,640]{0,1:T(8,128)(2,1)S(1)} %fusion.24), kind=kOutput, calls=%fused_computation.29 | convolution fusion | flops 8390656000 | bytes 19824640 | tf_op jit(solution)/shard_map/dot_general | solution.py:377
  484.5 33.8 %fusion.1 = (bf16[2048,3200]{0,1:T(8,128)(2,1)}, bf16[2048,3200]{0,1:T(8,128)(2,1)}) fusion(f32[2048,3200]{0,1:T(8,128)} %get-tuple-element.59, f32[2048,3200]{0,1:T(8,128)} %fusion.39, bf16[3200,640]{1,0:T(8,128)(2,1)} %bitcast.127, bf16[2048,640]{0,1:T(8,128)(2,1)} %copy-done.2), kind=kOutput, calls=%fused_computation.3 | convolution fusion | flops 8486912000 | bytes 85360640 | tf_op jit(solution)/shard_map/dot_general | solution.py:377
  518.3 14.2 %convolution_convert_fusion.6 = bf16[640,3200]{1,0:T(8,128)(2,1)} fusion(bf16[2048,3200]{0,1:T(8,128)(2,1)} %get-tuple-element.36, bf16[1,2048,640]{1,2,0:T(8,128)(2,1)S(1)} %copy-done.1, f32[2048]{0:T(1024)S(1)} %copy-done.16), kind=kOutput, calls=%fused_computation.34 | convolution fusion | flops 8394588160 | bytes 19832832 | tf_op jit(solution)/shard_map/dot_general | solution.py:377
  532.4 14.2 %convolution_convert_fusion.5 = bf16[640,3200]{1,0:T(8,128)(2,1)} fusion(bf16[2048,3200]{0,1:T(8,128)(2,1)} %get-tuple-element.37, bf16[1,2048,640]{1,2,0:T(8,128)(2,1)S(1)} %copy-done.1, f32[2048]{0:T(1024)S(1)} %copy-done.16), kind=kOutput, calls=%fused_computation.33 | convolution fusion | flops 8394588160 | bytes 19832832 | tf_op jit(solution)/shard_map/dot_general | solution.py:377
  546.6 76.4 %xy_scatter.2 = (f32[40,3200]{1,0:T(8,128)}, f32[40,3200]{1,0:T(8,128)}, f32[200,640]{1,0:T(8,128)}) custom-call(bf16[4,4,40,3200]{3,2,1,0:T(8,128)(2,1)} %bitcast.123, bf16[4,4,40,3200]{3,2,1,0:T(8,128)(2,1)} %bitcast.125, bf16[4,4,200,640]{3,2,1,0:T(8,128)(2,1)} %bitcast.120), custom_call_target="tpu_custom_call" | custom-call | tf_op jit(solution)/shard_map/xy_scatter/pallas_call | solution.py:293
  623.0 2.0 reshape.115
  626.9 1.9 reshape.116
  639.2 23.7 %z_scatter.1 = bf16[6,128,128]{2,1,0:T(8,128)(2,1)} custom-call(f32[8,6,128,128]{3,2,1,0:T(8,128)} %bitcast_dynamic-update-slice_fusion.own), custom_call_target="tpu_custom_call" | custom-call | tf_op jit(solution)/shard_map/z_scatter/pallas_call | solution.py:337
  666.5 13.3 %convolution_convert_fusion.7 = bf16[2048,640]{0,1:T(8,128)(2,1)S(1)} fusion(bf16[640,3200]{1,0:T(8,128)(2,1)} %bitcast.114, bf16[2048,3200]{0,1:T(8,128)(2,1)} %get-tuple-element.37), kind=kOutput, calls=%fused_computation.46 | convolution fusion | flops 8389918720 | bytes 19824640 | tf_op jit(solution)/shard_map/dot_general | solution.py:377
  679.9 12.4 %fusion.15 = (f32[2048]{0:T(1024)S(1)}, bf16[2048,640]{0,1:T(8,128)(2,1)S(1)}) fusion(bf16[1,2048,640]{1,2,0:T(8,128)(2,1)S(1)} %copy-done.1, bf16[2048,640]{0,1:T(8,128)(2,1)S(1)} %convolution_convert_fusion.7, bf16[640,3200]{1,0:T(8,128)(2,1)S(1)} %bitcast.113, bf16[2048,3200]{0,1:T(8,128)(2,1)} %get-tuple-element.36), kind=kOutput, calls=%fused_computation.40 | convolution fusion | flops 8396470272 | bytes 25075712 | tf_op jit(solution)/shard_map/dot_general | solution.py:377
  692.3 3.3 fusion.23
  695.6 4.4 copy.52
  (87 shorter events, 27.8 us)
Async XLA Ops:
  4.7 0.7 copy-start.12
  172.3 51.5 %copy-start = (bf16[1,2048,640]{1,2,0:T(8,128)(2,1)}, bf16[1,2048,640]{1,2,0:T(8,128)(2,1)S(1)}, u32[]{:S(2)}) copy-start(bf16[1,2048,640]{1,2,0:T(8,128)(2,1)S(1)} %copy.32) | copy-start | bytes 7864324
  172.8 1.0 copy-start.13
  173.8 18.2 %copy-start.15 = (f32[2048]{0:T(1024)}, f32[2048]{0:T(1024)S(1)}, u32[]{:S(2)}) copy-start(f32[2048]{0:T(1024)S(1)} %add_rsqrt_fusion.1) | copy-start | bytes 24580
  173.8 18.2 %copy-start.5 = (bf16[1,4,4,40,3200]{4,3,2,1,0:T(8,128)(2,1)S(1)}, bf16[1,4,4,40,3200]{4,3,2,1,0:T(8,128)(2,1)}, u32[]{:S(2)}) copy-start(bf16[1,4,4,40,3200]{4,3,2,1,0:T(8,128)(2,1)} %get-tuple-element.67) | copy-start | bytes 12288004
  223.7 14.5 %copy-start.8 = (bf16[1,4,4,200,640]{4,3,2,1,0:T(8,128)(2,1)}, bf16[1,4,4,200,640]{4,3,2,1,0:T(8,128)(2,1)S(1)}, u32[]{:S(2)}) copy-start(bf16[1,4,4,200,640]{4,3,2,1,0:T(8,128)(2,1)S(1)} %get-tuple-element.41) | copy-start | bytes 12288004
  223.8 14.6 %copy-start.6 = (bf16[1,4,4,40,3200]{4,3,2,1,0:T(8,128)(2,1)S(1)}, bf16[1,4,4,40,3200]{4,3,2,1,0:T(8,128)(2,1)}, u32[]{:S(2)}) copy-start(bf16[1,4,4,40,3200]{4,3,2,1,0:T(8,128)(2,1)} %get-tuple-element.42) | copy-start | bytes 12288004
  238.3 14.0 %copy-start.9 = (bf16[2048,640]{0,1:T(8,128)(2,1)}, bf16[2048,640]{0,1:T(8,128)(2,1)S(1)}, u32[]{:S(2)}) copy-start(bf16[2048,640]{0,1:T(8,128)(2,1)S(1)} %get-tuple-element.61) | copy-start | bytes 7864324
  238.3 14.0 %copy-start.17 = (f32[2048]{0:T(1024)}, f32[2048]{0:T(1024)S(1)}, u32[]{:S(2)}) copy-start(f32[2048]{0:T(1024)S(1)} %get-tuple-element.60) | copy-start | bytes 24580
  252.3 14.9 %copy-start.10 = (bf16[2048,640]{0,1:T(8,128)(2,1)S(1)}, bf16[2048,640]{0,1:T(8,128)(2,1)}, u32[]{:S(2)}) copy-start(bf16[2048,640]{0,1:T(8,128)(2,1)} %copy-done.9) | copy-start | bytes 7864324
  434.4 13.5 %copy-start.7 = (bf16[1,4,4,40,3200]{4,3,2,1,0:T(8,128)(2,1)S(1)}, bf16[1,4,4,40,3200]{4,3,2,1,0:T(8,128)(2,1)}, u32[]{:S(2)}) copy-start(bf16[1,4,4,40,3200]{4,3,2,1,0:T(8,128)(2,1)} %get-tuple-element.42) | copy-start | bytes 12288004
  448.0 13.4 %copy-start.18 = (f32[2048]{0:T(1024)S(1)}, f32[2048]{0:T(1024)}, u32[]{:S(2)}) copy-start(f32[2048]{0:T(1024)} %copy-done.17) | copy-start | bytes 24580
  468.7 15.8 %copy-start.2 = (bf16[2048,640]{0,1:T(8,128)(2,1)}, bf16[2048,640]{0,1:T(8,128)(2,1)S(1)}, u32[]{:S(2)}) copy-start(bf16[2048,640]{0,1:T(8,128)(2,1)S(1)} %fusion.24) | copy-start | bytes 7864324
  484.5 33.8 %copy-start.1 = (bf16[1,2048,640]{1,2,0:T(8,128)(2,1)S(1)}, bf16[1,2048,640]{1,2,0:T(8,128)(2,1)}, u32[]{:S(2)}) copy-start(bf16[1,2048,640]{1,2,0:T(8,128)(2,1)} %copy-done) | copy-start | bytes 7864324
  484.5 33.8 %copy-start.16 = (f32[2048]{0:T(1024)S(1)}, f32[2048]{0:T(1024)}, u32[]{:S(2)}) copy-start(f32[2048]{0:T(1024)} %copy-done.15) | copy-start | bytes 24580
  623.0 11.5 %copy-start.11 = (f32[8,125,128]{2,1,0:T(8,128)S(1)}, f32[8,125,128]{2,1,0:T(8,128)}, u32[]{:S(2)}) copy-start(f32[8,125,128]{2,1,0:T(8,128)} %reshape.121) | copy-start | bytes 1536004
  666.5 13.3 %copy-start.4 = (bf16[1,4,4,40,3200]{4,3,2,1,0:T(8,128)(2,1)S(1)}, bf16[1,4,4,40,3200]{4,3,2,1,0:T(8,128)(2,1)}, u32[]{:S(2)}) copy-start(bf16[1,4,4,40,3200]{4,3,2,1,0:T(8,128)(2,1)} %get-tuple-element.68) | copy-start | bytes 12288004
  679.8 12.4 %copy-start.14 = (f32[2048]{0:T(1024)S(1)}, f32[2048]{0:T(1024)}, u32[]{:S(2)}) copy-start(f32[2048]{0:T(1024)} %copy-done.13) | copy-start | bytes 24580
  679.8 12.5 %copy-start.3 = (bf16[2048,640]{0,1:T(8,128)(2,1)S(1)}, bf16[2048,640]{0,1:T(8,128)(2,1)}, u32[]{:S(2)}) copy-start(bf16[2048,640]{0,1:T(8,128)(2,1)} %copy-done.2) | copy-start | bytes 7864324

commit v3 on v2

--- a/solution.py
+++ b/solution.py
@@ -108,7 +108,7 @@
 
 def cut_rows(ref):
     lead = ref.shape[0]
-    cut = 2 if len(ref.shape) == 3 else -(-lead // 16) * 8
+    cut = -(-lead // 2) if len(ref.shape) > 2 else -(-lead // 16) * 8
     return ref.at[pl.ds(0, cut)], ref.at[pl.ds(cut, lead - cut)]
 
 
@@ -199,106 +199,329 @@
     )(*owns)
 
 
-def each_block(fn, lead):
-    if lead is None:
-        fn(())
+def add_up(dst, parts):
+    lead = dst.shape[:-2]
+
+    def block(at):
+        total = parts[0][at].astype(F32)
+        for part in parts[1:]:
+            total += part[at].astype(F32)
+        dst[at] = total.astype(dst.dtype)
+
+    if not lead:
+        block(...)
+    elif len(lead) == 1:
+        pl.loop(0, lead[0])(lambda i: block(i))
     else:
-        pl.loop(0, lead)(lambda i: fn((i,)))
-
-
-def add_up(dst, parts):
-    lead = dst.shape[0] if len(dst.shape) == 3 else None
-
-    def block(at):
-        total = parts[0][at].astype(F32) if at else parts[0][...].astype(F32)
-        for part in parts[1:]:
-            total += (part[at] if at else part[...]).astype(F32)
-        if at:
-            dst[at] = total.astype(dst.dtype)
-        else:
-            dst[...] = total.astype(dst.dtype)
-
-    each_block(block, lead)
-
-
-def scatter_half(copies, term, exact, buffers, pos, right, left, dst):
+        pl.loop(0, lead[0])(lambda i: [block((i, j)) for j in range(lead[1])] and None)
+
+
+def scatter_phase(send, recv, term, exact, buffers, pos, right, left, finish):
     far_l, far_r, near_l, near_r, out_l, out_r = buffers
     ahead, behind = turn(pos, 1, SIDE), turn(pos, -1, SIDE)
     far0, far1 = cut_rows(term(turn(pos, 2, SIDE)))
     after0, before1 = cut_rows(term(ahead))[0], cut_rows(term(behind))[1]
+    before0, after1, own = cut_rows(exact(behind))[0], cut_rows(exact(ahead))[1], exact(pos)
     (nl0, nl1), (nr0, nr1) = map(cut_rows, (near_l, near_r))
-    to_left = copies.start(far0, far_r, left)
-    to_right = copies.start(far1, far_l, right)
-    plain = [copies.start(after0, nl0, right), copies.start(before1, nr1, left)]
-    yield
-    to_left.wait_recv()
-    add_up(out_l, (cut_rows(exact(behind))[0], far_r))
-    plain.append(copies.start(out_l, nr0, left))
-    to_right.wait_recv()
-    add_up(out_r, (cut_rows(exact(ahead))[1], far_l))
-    plain.append(copies.start(out_r, nl1, right))
-    yield
-    for copy in plain:
-        copy.wait_recv()
-    add_up(dst, (exact(pos), near_l, near_r))
-
-
-SCATTER_COPIES = 2 * 6
-
-
-def scatter_job(copies, ref, order, ring, first, total, cast, second, out):
+    pairs = ((far0, far_r, left), (far1, far_l, right), (after0, nl0, right), (before1, nr1, left), (out_l, nr0, left), (out_r, nl1, right))
+    copies = [
+        pltpu.make_async_remote_copy(src, dst, send(k), recv(k), device_id=peer, device_id_type=MESH) for k, (src, dst, peer) in enumerate(pairs)
+    ]
+
+    def first():
+        for copy in copies[:4]:
+            copy.start()
+
+    def second():
+        copies[0].wait_recv()
+        add_up(out_l, (before0, far_r))
+        copies[4].start()
+        copies[1].wait_recv()
+        add_up(out_r, (after1, far_l))
+        copies[5].start()
+
+    def third():
+        for copy in copies[2:]:
+            copy.wait_recv()
+        finish((own, near_l, near_r))
+        for copy in copies:
+            copy.wait_send()
+
+    return first, second, third
+
+
+def unit_scratch(rows, cols):
+    whole = (SIDE, *rows, cols)
+    half = (SIDE // 2, *rows, cols)
+    cut = -(-rows[0] // 2) if len(rows) > 1 else -(-rows[0] // 16) * 8
+    top, low = (cut, *rows[1:], cols), (rows[0] - cut, *rows[1:], cols)
+    two = lambda shape: VMEM((2, *shape), BF16)
+    near = (*rows, cols)
+    first = [two(half), two(half), two(whole), two(whole), VMEM(half, BF16), VMEM(half, BF16)]
+    second = [two(low), two(top), two(near), two(near), VMEM(top, BF16), VMEM(low, BF16)]
+    return [*first, *second, VMEM((2, *whole), F32), two(whole)]
+
+
+def unit_phases(kind, order, ring, sems, scratch, term, slot1, slot2, out):
     x, y, xr, xl, yr, yl = ring
-    along_x, along_y = (x, xr, xl), (y, yr, yl)
-    if order == 0:
-        one, two, term = along_x, along_y, lambda i: ref.at[i]
-    else:
-        one, two, term = along_y, along_x, lambda i: ref.at[:, i]
-    yield from scatter_half(copies, term, term, first, *one, total)
-
-    @pl.loop(0, SIDE)
-    def _(i):
-        cast[i] = total[i].astype(BF16)
-
-    yield from scatter_half(copies, lambda i: cast.at[i], lambda i: total.at[i], second, *two, out)
-
-
-def scatter_scratch(rows, cols):
-    cut = -(-rows // 16) * 8
-    half, whole = VMEM((2, rows, cols), BF16), VMEM((SIDE, rows, cols), BF16)
-    near, top, low = VMEM((rows, cols), BF16), VMEM((cut, cols), BF16), VMEM((rows - cut, cols), BF16)
-    first = [half, half, whole, whole, half, half]
-    second = [low, top, near, near, top, low]
-    return [*first, VMEM((SIDE, rows, cols), F32), whole, *second]
-
-
-def xy_scatter_kernel(depth, *refs):
-    ins, outs, (send, recv), scratch = refs[:3], refs[3:6], refs[6:8], refs[8:]
+    rings = ((x, xr, xl), (y, yr, yl))
+    one, two = rings[order], rings[1 - order]
+    region = (lambda i: term.at[i]) if order == 0 else (lambda i: term.at[:, i])
+    total, cast = scratch[12:]
+    send, recv = sems
+
+    def buffers(k, slot):
+        return [ref.at[slot] for ref in scratch[k : k + 4]] + list(scratch[k + 4 : k + 6])
+
+    def keep(parts):
+        add_up(total.at[slot1], parts)
+        add_up(cast.at[slot1], (total.at[slot1],))
+
+    def give(parts):
+        add_up(out, parts)
+
+    sem = lambda which, phase, slot: lambda k: which.at[kind, phase, slot, k]
+    phase1 = scatter_phase(sem(send, 0, slot1), sem(recv, 0, slot1), region, region, buffers(0, slot1), *one, keep)
+    phase2 = scatter_phase(
+        sem(send, 1, slot2), sem(recv, 1, slot2), lambda i: cast.at[slot2, i], lambda i: total.at[slot2, i], buffers(6, slot2), *two, give
+    )
+    return phase1, phase2
+
+
+CHUNK, TILE = 640, 512
+
+
+def dot(a, b, ca=1, cb=0):
+    return lax.dot_general(a, b, (((ca,), (cb,)), ((), ())), preferred_element_type=F32)
+
+
+def scale_of(wide):
+    return lax.rsqrt(jnp.mean(wide**2, -1, keepdims=True) + 1e-6)
+
+
+def backward_kernel(depth, h0, h1, dy, p0, gu0, gu1, down, dx, sum_gu, sum_d, *scratch):
+    (h, a, a_t, d, d_t, da, p, dg, du, w, gu_terms, d_terms), scratch = scratch[:12], scratch[12:]
+    (load, load_w, send, recv), units = scratch[:4], scratch[4:]
+    gu_units, d_units = (units[:14], units[14:28]), (units[28:42], units[42:])
+    tokens, width = h.shape
+    chunks = gu0.shape[2] // CHUNK
+    blocks = d_terms.shape[3]
+    rows = d_terms.shape[4]
     _, ring = neighbours(depth)
-    meet(ring[2:-1])
-    copies = Copies(send, recv)
-    jobs = []
-    for ref, out in zip(ins, outs):
-        for which in range(2):
-            mine, scratch = scratch[:14], scratch[14:]
-            cols = columns(ref.shape[-1])[which]
-            jobs.append(scatter_job(copies, ref.at[:, :, :, cols], which, ring[:-1], mine[:6], mine[6], mine[7], mine[8:], out.at[:, cols]))
-    run_together(jobs)
-    copies.drain()
-
-
-def xy_scatter(terms, depth, cid):
-    scratch = [DMA((6 * SCATTER_COPIES,)), DMA((6 * SCATTER_COPIES,))]
-    for term in terms:
-        scratch += [spec for cols in columns(term.shape[-1]) for spec in scatter_scratch(term.shape[2], cols.size)]
+    ring = ring[:-1]
+    meet(ring[2:])
+
+    def weights(gu, layer, c, slot):
+        cols = pl.ds(pl.multiple_of(c * CHUNK, CHUNK), CHUNK)
+        sources = (gu.at[0, :, cols], gu.at[1, :, cols], down.at[layer, cols, :])
+        return [pltpu.make_async_copy(src, w.at[slot, k], load_w.at[slot, k]) for k, src in enumerate(sources)]
+
+    def prepare(h_hbm, d_hbm):
+        copies = [pltpu.make_async_copy(h_hbm, h, load.at[0])]
+        if d_hbm is not None:
+            copies.append(pltpu.make_async_copy(d_hbm, d, load.at[1]))
+        for copy in copies:
+            copy.start()
+        for copy in copies:
+            copy.wait()
+
+        @pl.loop(0, tokens // 256)
+        def _(t):
+            at = pl.ds(pl.multiple_of(t * 256, 256), 256)
+            wide = h[at].astype(F32)
+            normed = (wide * scale_of(wide)).astype(BF16)
+            a[at] = normed
+            a_t[:, at] = normed.T
+            d_t[:, at] = d[at].T
+            da[at] = jnp.zeros((256, width), F32)
+
+    def finish():
+        @pl.loop(0, tokens // 256)
+        def _(t):
+            at = pl.ds(pl.multiple_of(t * 256, 256), 256)
+            wide = h[at].astype(F32)
+            scale = scale_of(wide)
+            by_a = da[at].astype(BF16).astype(F32)
+            inner = jnp.mean(by_a * wide, -1, keepdims=True)
+            by_h = (by_a * scale - wide * (scale * scale * scale * inner)).astype(BF16)
+            d[at] = (d[at].astype(F32) + by_h.astype(F32)).astype(BF16)
+
+    def down_term(layer, c):
+        term = dot(d_t[...], p[...]).T
+        for m in range(CHUNK // rows):
+            g = c * (CHUNK // rows) + m
+            d_terms[layer, g // (blocks * SIDE), lax.rem(g // blocks, SIDE), lax.rem(g, blocks)] = term[m * rows : (m + 1) * rows].astype(BF16)
+
+    def tile(t, slot):
+        at = pl.ds(pl.multiple_of(t * TILE, TILE), TILE)
+        a_here = a[at]
+        gate, up = dot(a_here, w[slot, 0]), dot(a_here, w[slot, 1])
+        by_p = dot(d[at], w[slot, 2], 1, 1).astype(BF16).astype(F32)
+        sig = jax.nn.sigmoid(gate)
+        act = gate * sig
+        p[at] = (act * up).astype(BF16)
+        by_gate = (by_p * up * (sig + act * (1 - sig))).astype(BF16)
+        by_up = (by_p * act).astype(BF16)
+        dg[at] = by_gate
+        du[at] = by_up
+        da[at] += dot(by_gate, w[slot, 0], 1, 1) + dot(by_up, w[slot, 1], 1, 1)
+
+    def gate_up_terms(slot):
+        for k, by in enumerate((dg, du)):
+            term = dot(a_t[...], by[...])
+            count = SIDE * SIDE
+            for b in range(count):
+                n = width // count
+                gu_terms[slot, k, b // SIDE, b % SIDE] = term[b * n : (b + 1) * n].astype(BF16)
+
+    def gu_phases(slot1, slot2, layer, c):
+        cols = pl.ds(pl.multiple_of(c * CHUNK, CHUNK), CHUNK)
+        return [
+            unit_phases(k, k, ring, (send, recv), gu_units[k], gu_terms.at[slot1, k], slot1, slot2, sum_gu.at[layer, k, :, cols]) for k in range(2)
+        ]
+
+    def d_phases(c):
+        here, last = lax.rem(c, 2), lax.rem(c + 1, 2)
+        cols, before = (pl.ds(pl.multiple_of(k * 128, 128), 128) for k in (c, jnp.maximum(c - 1, 0)))
+        return [
+            unit_phases(2 + k, k, ring, (send, recv), d_units[k], d_terms.at[k, :, :, :, :, cols], here, last, sum_d.at[k, :, :, before]) for k in range(2)
+        ]
+
+    def segment(k, phases, condition=None):
+        def run():
+            for phase in phases:
+                phase[k]()
+
+        if condition is None:
+            run()
+        else:
+            pl.when(condition)(run)
+
+    for copy in weights(gu1, 1, 0, 0):
+        copy.start()
+    prepare(h1, dy)
+
+    @pl.loop(0, chunks)
+    def _(c):
+        slot, other = lax.rem(c, 2), lax.rem(c + 1, 2)
+        for copy in weights(gu1, 1, c, slot):
+            copy.wait()
+
+        @pl.when(c < chunks - 1)
+        def _():
+            for copy in weights(gu1, 1, jnp.minimum(c + 1, chunks - 1), other):
+                copy.start()
+
+        @pl.when(c == chunks - 1)
+        def _():
+            for copy in weights(gu0, 0, 0, other):
+                copy.start()
+
+        phases = gu_phases(other, slot, 1, jnp.maximum(c - 2, 0))
+        ones, twos = zip(*phases)
+        segment(0, ones, c > 0)
+        segment(0, twos, c > 1)
+
+        @pl.loop(0, tokens // TILE)
+        def _(t):
+            tile(t, slot)
+            segment(1, twos, (c > 1) & (t == 0))
+            segment(1, ones, (c > 0) & (t == 1))
+
+        gate_up_terms(slot)
+        down_term(1, c)
+        segment(2, ones, c > 0)
+        segment(2, twos, c > 1)
+
+    finish()
+    prepare(h0, None)
+
+    @pl.loop(0, chunks)
+    def _(c):
+        copy = pltpu.make_async_copy(p0.at[:, pl.ds(pl.multiple_of(c * CHUNK, CHUNK), CHUNK)], p, load.at[0])
+        copy.start()
+        copy.wait()
+        down_term(0, c)
+
+    first = chunks % 2
+
+    @pl.loop(0, chunks)
+    def _(c):
+        slot, other = lax.rem(c + first, 2), lax.rem(c + first + 1, 2)
+        for copy in weights(gu0, 0, c, slot):
+            copy.wait()
+
+        @pl.when(c < chunks - 1)
+        def _():
+            for copy in weights(gu0, 0, jnp.minimum(c + 1, chunks - 1), other):
+                copy.start()
+
+        late = jnp.where(c < 2, 1, 0)
+        phases = gu_phases(other, slot, late, lax.rem(c - 2 + chunks, chunks))
+        (ones, twos), (d_ones, d_twos) = zip(*phases), zip(*d_phases(c))
+        segment(0, ones)
+        segment(0, twos)
+        segment(0, d_ones)
+        segment(0, d_twos, c > 0)
+
+        @pl.loop(0, tokens // TILE)
+        def _(t):
+            tile(t, slot)
+            segment(1, twos, t == 1)
+            segment(1, ones, t == 1)
+            segment(1, d_ones, t == 3)
+            segment(1, d_twos, (t == 3) & (c > 0))
+
+        gate_up_terms(slot)
+        segment(2, ones)
+        segment(2, twos)
+        segment(2, d_ones)
+        segment(2, d_twos, c > 0)
+
+    slot, other = (first + chunks) % 2, (first + chunks + 1) % 2
+    ones, twos = zip(*gu_phases(other, slot, 0, chunks - 2))
+    _, d_twos = zip(*d_phases(jnp.int32(chunks)))
+    for k in range(3):
+        segment(k, ones)
+        segment(k, twos)
+        segment(k, d_twos)
+        if k == 0:
+            finish()
+            save = pltpu.make_async_copy(d, dx, load.at[0])
+            save.start()
+    save.wait()
+    _, twos = zip(*gu_phases(slot, other, 0, chunks - 1))
+    for k in range(3):
+        segment(k, twos)
+
+
+def backward(h0, h1, dy, p0, gu0, gu1, down, depth, cid):
+    tokens, width = h0.shape
+    ff = p0.shape[1]
+    rows = width // SIDE**2
+    blocks = ff // width
+    assert blocks * 128 == width and blocks * CHUNK == ff and tokens % TILE == 0
+    act = VMEM((tokens, width), BF16)
+    scratch = [act, act, VMEM((width, tokens), BF16), act, VMEM((width, tokens), BF16), VMEM((tokens, width), F32)]
+    scratch += [VMEM((tokens, CHUNK), BF16)] * 3 + [VMEM((2, 3, width, CHUNK), BF16)]
+    scratch += [VMEM((2, 2, SIDE, SIDE, rows, CHUNK), BF16), VMEM((2, SIDE, SIDE, blocks, rows, width), BF16)]
+    scratch += [DMA((2,)), DMA((2, 3)), DMA((4, 2, 2, 6)), DMA((4, 2, 2, 6))]
+    scratch += unit_scratch((rows,), CHUNK) * 2 + unit_scratch((blocks, rows), 128) * 2
+    hbm = pl.BlockSpec(memory_space=pl.ANY)
+    vmem = pl.BlockSpec(memory_space=VMEM)
     return pl.pallas_call(
-        functools.partial(xy_scatter_kernel, depth),
-        out_shape=[jax.ShapeDtypeStruct(term.shape[2:], F32) for term in terms],
-        in_specs=[pl.BlockSpec(memory_space=VMEM)] * 3,
-        out_specs=[pl.BlockSpec(memory_space=VMEM)] * 3,
+        functools.partial(backward_kernel, depth),
+        out_shape=[
+            jax.ShapeDtypeStruct((tokens, width), BF16),
+            jax.ShapeDtypeStruct((2, 2, rows, ff), F32),
+            jax.ShapeDtypeStruct((2, blocks, rows, width), F32),
+        ],
+        in_specs=[hbm] * 7,
+        out_specs=[hbm, vmem, vmem],
         scratch_shapes=scratch,
-        compiler_params=pltpu.CompilerParams(collective_id=cid, has_side_effects=True, vmem_limit_bytes=60 << 20),
-        name="xy_scatter",
-    )(*terms)
+        compiler_params=pltpu.CompilerParams(collective_id=cid, has_side_effects=True, vmem_limit_bytes=67043328),
+        name="backward",
+    )(h0, h1, dy, p0, gu0, gu1, down)
 
 
 def z_scatter_kernel(depth, parts, own, out, in_r, out_r, in_l, out_l, send, recv):
@@ -373,39 +596,6 @@
     return [unflat(out[k], shape) for k, shape in enumerate(shapes)]
 
 
-def dot(a, b, ca, cb):
-    return lax.dot_general(a, b, (((ca,), (cb,)), ((), ())), preferred_element_type=F32)
-
-
-def norm_parts(h):
-    wide = h.astype(F32)
-    scale = lax.rsqrt(jnp.mean(wide**2, -1, keepdims=True) + 1e-6)
-    return wide, scale
-
-
-def forward(h, wg, wu, wd, last):
-    wide, scale = norm_parts(h)
-    a = (wide * scale).astype(BF16)
-    gate, up = dot(a, wg, 1, 0), dot(a, wu, 1, 0)
-    p = (jax.nn.silu(gate) * up).astype(BF16)
-    out = None if last else h + dot(p, wd, 1, 0).astype(BF16)
-    return out, (wide, scale, a, gate, up, p)
-
-
-def backward(d, saved, wg, wu, wd):
-    wide, scale, a, gate, up, p = saved
-    dp = dot(d, wd, 1, 1).astype(BF16).astype(F32)
-    dwd = dot(p, d, 0, 0).astype(BF16)
-    sig = jax.nn.sigmoid(gate)
-    dg = (dp * up * (sig * (1 + gate * (1 - sig)))).astype(BF16)
-    du = (dp * gate * sig).astype(BF16)
-    dwg, dwu = dot(a, dg, 0, 0).astype(BF16), dot(a, du, 0, 0).astype(BF16)
-    da = (dot(dg, wg, 1, 1).astype(BF16) + dot(du, wu, 1, 1).astype(BF16)).astype(F32)
-    inner = jnp.sum(da * wide, -1, keepdims=True) / wide.shape[-1]
-    dwide = da * scale - wide * (scale**3 * inner)
-    return d + dwide.astype(BF16), dwg, dwu, dwd
-
-
 def solution(mesh):
     n = mesh.shape["dp"]
     depth = n // SIDE**2
@@ -413,17 +603,15 @@
     def step(x, dy, wg, wu, wd):
         d_model, ff = wg.shape[1] * n, wg.shape[2]
         gu0, gu1, down = gather_weights(wg, wu, wd, depth)
-        wg0, wu0, wg1, wu1 = (t.reshape(d_model, ff) for t in (*gu0, *gu1))
-        wd0, wd1 = (t.reshape(ff, d_model) for t in down)
-        h1, saved0 = forward(x[0], wg0, wu0, wd0, False)
-        _, saved1 = forward(h1, wg1, wu1, wd1, True)
-        dh, *terms1 = backward(dy[0], saved1, wg1, wu1, wd1)
-        dh, *terms0 = backward(dh, saved0, wg0, wu0, wd0)
-        sums = []
-        for k, terms in enumerate((terms0, terms1)):
-            sums += xy_scatter([t.reshape(SIDE, SIDE, -1, t.shape[1]) for t in terms], depth, 3 + k)
+        gu0, gu1, down = gu0.reshape(2, d_model, ff), gu1.reshape(2, d_model, ff), down.reshape(2, ff, d_model)
+        wide = x[0].astype(F32)
+        normed = (wide * scale_of(wide)).astype(BF16)
+        p0 = (jax.nn.silu(dot(normed, gu0[0])) * dot(normed, gu0[1])).astype(BF16)
+        h1 = x[0] + dot(p0, down[0]).astype(BF16)
+        dx, sum_gu, sum_d = backward(x[0], h1, dy[0], p0, gu0, gu1, down, depth, 3)
+        sums = [*sum_gu[0], sum_d[0], *sum_gu[1], sum_d[1]]
         g0, u0, d0, g1, u1, d1 = scatter_grads(sums, [t.shape[1:] for t in (wg, wu, wd)] * 2, depth)
-        return dh[None], jnp.stack([g0, g1]), jnp.stack([u0, u1]), jnp.stack([d0, d1])
+        return dx[None], jnp.stack([g0, g1]), jnp.stack([u0, u1]), jnp.stack([d0, d1])
 
     data = P(("rep", "dp"), None, None)
     weight = P(None, "dp", None)

time: 706 us -> 537 us (0.76)
  matrix products: 309 us -> 48.3 us
  Pallas kernels: 322 us -> 433 us
  local copies, waits for them, and re-layouts: 54.7 us -> 43.8 us
  other arithmetic: 13.1 us -> 4.85 us
    dot_general x17 -> x3, matrix products: 309 us -> 48.3 us  [dot(): lax.dot_general(a, b, (((ca,), (cb,)), ((), ())), preferred_element_type=...]
    pallas_call x2 -> x1, Pallas kernels: 152 us -> 267 us  [backward(): pl.pallas_call(functools.partial(backward_kernel, depth), out_shape=[jax....]
    slice x0 -> x3, local copies, waits for them, and re-layouts: none -> 10.1 us  [the longest x1 5.33 us: step(): p0 = (jax.nn.silu(dot(normed, gu0[0])) * dot(normed, gu0[1])).astype(BF16)]
    reshape x6 -> x0, local copies, waits for them, and re-layouts: 9.97 us -> none  [scatter_grads(): t = t.reshape(depth, -1, 128)]
    unnamed x51 -> x17, local copies, waits for them, and re-layouts: 19.4 us -> 11.2 us
    another operation x2 -> x7, local copies, waits for them, and re-layouts: 16.1 us -> 13.1 us  [the longest x6 10.4 us: scatter_grads(): t = t.reshape(depth, -1, 128)]
where the time goes in v3:
time: 537 us; the launch traced here: 531 us
  Pallas kernels  433 us (81%)
  matrix products  48.3 us (9%)
  local copies, waits for them, and re-layouts  43.8 us (8%)
    pallas_call x1, Pallas kernels, backward(): pl.pallas_call(functools.partial(backward_kernel, depth), out_shape=[jax....  267 us
    pallas_call x1, Pallas kernels, xy_gather(): pl.pallas_call(functools.partial(xy_gather_kernel, depth), out_shape=[jax...  124 us
    dot_general x3, matrix products, dot(): lax.dot_general(a, b, (((ca,), (cb,)), ((), ())), preferred_element_type=...  48.3 us
    pallas_call x1, Pallas kernels, z_gather(): pl.pallas_call(functools.partial(z_gather_kernel, depth, parts), out_shap...  21.7 us
    pallas_call x1, Pallas kernels, z_scatter(): pl.pallas_call(functools.partial(z_scatter_kernel, depth, parts), out_sha...  20.2 us
    unnamed x17, local copies, waits for them, and re-layouts  11.2 us

profile of v3, /device:TPU:32, one launch (start us, length us, event | category | flops | bytes accessed | tf_op | source)
XLA Modules:
  0.0 531.4 jit_solution(862706433776442480)
XLA Ops:
  0.6 1.2 slice_reduce_fusion.4
  2.0 1.2 slice_reduce_fusion
  3.3 1.2 slice_reduce_fusion.1
  5.4 21.7 %z_gather.1 = bf16[8,6,128,128]{3,2,1,0:T(8,128)(2,1)} custom-call(bf16[6,128,128]{2,1,0:T(8,128)(2,1)} %copy-done.2), custom_call_target="tpu_custom_call" | custom-call | tf_op jit(solution)/shard_map/z_gather/pallas_call | solution.py:93
  27.1 1.5 slice_bitcast_fusion.1
  29.8 1.1 pad_maximum_fusion
  31.3 0.9 pad_maximum_fusion.2.own2
  32.2 124.1 %xy_gather.1 = (bf16[2,4,4,40,3200]{4,3,2,1,0:T(8,128)(2,1)}, bf16[2,4,4,40,3200]{4,3,2,1,0:T(8,128)(2,1)}, bf16[2,4,4,200,640]{4,3,2,1,0:T(8,128)(2,1)}) custom-call(bf16[2,40,3200]{2,1,0:T(8,128)(2,1)} %get-tuple-element.42.own0, bf16[2,40,3200]{2,1,0:T(8,128)(2,1)} %get-tuple-element.43.own1, bf16[2,200,640]{2,1,0:T(8,128)(2,1)} %pad_maximum_fusion.2.own2), custom_call_target="tpu_custom_call" | custom-call | tf_op jit(solution)/shard_map/xy_gather/pallas_call | solution.py:191
  156.3 5.3 %fusion.5 = (bf16[1,4,4,40,3200]{4,3,2,1,0:T(8,128)(2,1)}, bf16[1,4,4,40,3200]{4,3,2,1,0:T(8,128)(2,1)S(1)}) fusion(bf16[2,4,4,40,3200]{4,3,2,1,0:T(8,128)(2,1)} %get-tuple-element.10), kind=kLoop, calls=%fused_computation.38 | loop fusion | bytes 16384000 | tf_op jit(solution)/shard_map/slice | solution.py:609
  162.2 14.6 %fusion.3 = f32[2048,3200]{1,0:T(8,128)} fusion(bf16[640,3200]{1,0:T(8,128)(2,1)S(1)} %bitcast.79, bf16[1,2048,640]{2,1,0:T(8,128)(2,1)S(1)} %copy-done, f32[2048]{0:T(1024)S(1)} %add_rsqrt_fusion), kind=kOutput, calls=%fused_computation.6 | convolution fusion | flops 8392540160 | bytes 32940032 | tf_op jit(solution)/shard_map/dot_general | solution.py:295
  176.8 19.0 %multiply_convert_fusion.p0 = bf16[2048,3200]{1,0:T(8,128)(2,1)} fusion(f32[2048,3200]{1,0:T(8,128)} %fusion.3, bf16[640,3200]{1,0:T(8,128)(2,1)} %bitcast.78, bf16[1,2048,640]{2,1,0:T(8,128)(2,1)S(1)} %copy-done, f32[2048]{0:T(1024)S(1)} %add_rsqrt_fusion), kind=kOutput, calls=%fused_computation | convolution fusion | flops 8431861760 | bytes 46047232 | tf_op jit(solution)/shard_map/dot_general | solution.py:295
  195.8 2.5 slice.138
  198.3 14.7 %fusion.1.h1 = bf16[2048,640]{1,0:T(8,128)(2,1)} fusion(bf16[2048,3200]{1,0:T(8,128)(2,1)} %multiply_convert_fusion.p0, bf16[3200,640]{1,0:T(8,128)(2,1)S(1)} %bitcast.77, bf16[1,2048,640]{2,1,0:T(8,128)(2,1)S(1)} %copy-done), kind=kOutput, calls=%fused_computation.5 | convolution fusion | flops 8391229440 | bytes 22446080 | tf_op jit(solution)/shard_map/dot_general | solution.py:295
  213.0 267.1 %backward.1 = (bf16[2048,640]{1,0:T(8,128)(2,1)}, f32[2,2,40,3200]{3,2,1,0:T(8,128)}, f32[2,5,40,640]{3,2,1,0:T(8,128)}) custom-call(bf16[2048,640]{1,0:T(8,128)(2,1)} %bitcast.75, bf16[2048,640]{1,0:T(8,128)(2,1)} %fusion.1.h1, bf16[2048,640]{1,0:T(8,128)(2,1)} %bitcast.80, bf16[2048,3200]{1,0:T(8,128)(2,1)} %multiply_convert_fusion.p0, ...), custom_call_target="tpu_custom_call" | custom-call | tf_op jit(solution)/shard_map/backward/pallas_call | solution.py:512
  480.1 2.7 fusion.6
  482.8 0.9 reshape_unstack.12
  483.7 1.1 bitcast_dynamic-update-slice_fusion.5
  484.8 1.9 reshape_unstack.13
  486.7 1.1 bitcast_dynamic-update-slice_fusion.4
  487.8 2.3 fusion.7
  490.1 1.9 reshape_squeeze.30
  491.9 1.1 bitcast_dynamic-update-slice_fusion.3
  493.0 1.9 reshape_unstack.14
  494.9 1.1 bitcast_dynamic-update-slice_fusion.2
  496.0 1.9 reshape_unstack.15
  497.9 1.1 bitcast_dynamic-update-slice_fusion.1
  499.0 1.9 reshape_squeeze.31
  500.9 1.1 bitcast_dynamic-update-slice_fusion.own
  502.0 1.7 copy-done.1
  503.7 20.2 %z_scatter.1 = bf16[6,128,128]{2,1,0:T(8,128)(2,1)} custom-call(f32[8,6,128,128]{3,2,1,0:T(8,128)} %copy-done.1), custom_call_target="tpu_custom_call" | custom-call | tf_op jit(solution)/shard_map/z_scatter/pallas_call | solution.py:560
  523.9 0.9 fusion.8
  527.5 3.5 copy.32
  (34 shorter events, 6.0 us)
Async XLA Ops:
  4.7 0.7 copy-start.2
  156.3 5.3 %copy-start = (bf16[1,2048,640]{2,1,0:T(8,128)(2,1)S(1)}, bf16[1,2048,640]{2,1,0:T(8,128)(2,1)}, u32[]{:S(2)}) copy-start(bf16[1,2048,640]{2,1,0:T(8,128)(2,1)} %param.5) | copy-start | bytes 7864324
  502.0 1.7 copy-start.1
